TPU v7x, 256 devices: a whole 4x4x8 slice. The times are simulated.
256 devices in a mesh: dp: 32 (over y, x, core), tensor: 8 (over z).
Axes of the slice: x: 4, y: 4, z: 8, core: 2. Of those that a mesh axis runs over, the one named last changes fastest.
Arguments:
- queries: bfloat16 [8192, 3072], P('dp', 'tensor'), may hold values from -96 to 96
- keys: bfloat16 [8192, 512], P('dp'), may hold values from -6 to 6
- values: bfloat16 [8192, 512], P('dp'), may hold values from -6 to 6
- lengths: int32 [16], replicated, may hold values from 1 to 6144, 8192 in all
- assignment: int32 [32, 32], replicated, may hold values from 0 to 31, each once within a row
- out_weight: bfloat16 [3072, 6144], P('tensor'), may hold values from -0.109375 to 0.109375
Outputs:
- mixed: bfloat16 [8192, 6144], P(('dp', 'tensor'))
Inputs may be any that keep to these rules, and one draw needn't show every extreme that they name: `lengths`: the prompts fill the 8192 positions in order, one of them exactly 6144 long. `assignment`: each row is a permutation of 0 to 31.
All inputs are finite; a program needn't handle non-finite values.
Results may differ from a plain program's by a relative error of at most 0.014.
Values may be sent and summed in bfloat16 or wider, within the bound.
No kernel may reach another device: no remote copies, remote signals or barrier semaphores. Data moves between devices by JAX's collectives and lax.ppermute only.
A program may use at most 64 MiB of HBM per device.

v0:
```python
import jax
import jax.numpy as jnp
from jax import lax
from jax.sharding import Mesh
from jax.sharding import PartitionSpec as P

HD = 128
HEADS = 24
KV_HEADS = 4
DP = ("dp_0", "dp_1", "dp_2")
DP_TENSOR = ("dp_0", "dp_1", "dp_2", "tensor")


def sent_together(arrays, axis, dim, along):
    ends, at = ([], 0)
    for a in arrays[:-1]:
        at += a.shape[along]
        ends.append(at)
    both = jnp.concatenate(arrays, axis=along)
    return tuple(jnp.split(lax.all_gather(both, axis, axis=dim, tiled=True), ends, axis=along))


def cut_along(value, dim, devices):
    before, after = (value.shape[:dim], value.shape[dim + 1 :])
    return jnp.moveaxis(value.reshape(*before, devices, -1, *after), dim, 0)


def laid_out(blocks, dim):
    dims = list(blocks.shape[1:])
    dims[dim] *= blocks.shape[0]
    return jnp.moveaxis(blocks, 0, dim).reshape(dims)


def moved_by_axis(blocks, axes, turns):
    inside = blocks.shape[1:]
    result = blocks.reshape(*(lax.axis_size(a) for a in axes), *inside)
    for k in turns:
        result = lax.all_to_all(result, axes[k], k, k, tiled=True)
    return result.reshape(-1, *inside)


def core_and_chips(value, groups, turns, split_dim, concat_dim):
    devices = lax.axis_size(groups[0]) * lax.axis_size(groups[1])
    blocks = cut_along(value, split_dim, devices)
    return laid_out(moved_by_axis(blocks, groups, turns), concat_dim)


def local(queries, keys, values, lengths, assignment, out_weight):
    n_groups = lax.axis_size(DP)
    my_group = lax.axis_index(DP)
    my_lane = lax.axis_index("tensor")
    tok_rows = queries.shape[0]
    q_width = queries.shape[1]
    heads_here = q_width // HD
    piece_rows = tok_rows // n_groups
    all_rows = tok_rows * n_groups
    score_scale = HD ** (-0.5)
    kv_head = my_lane * heads_here // (HEADS // KV_HEADS)
    own_keys = lax.dynamic_slice_in_dim(keys, kv_head * HD, HD, 1)
    own_values = lax.dynamic_slice_in_dim(values, kv_head * HD, HD, 1)
    doc_ends = jnp.cumsum(lengths)
    places = jnp.arange(all_rows, dtype=jnp.int32)
    doc_all = jnp.sum((places[:, None] >= doc_ends[None, :]).astype(jnp.int32), axis=1)

    def attend(softmax_state, query_rows, q_pos, q_doc, k_rows, v_rows, k_first):
        k_pos = k_first + jnp.arange(k_rows.shape[0], dtype=jnp.int32)
        k_doc = doc_all[jnp.clip(k_pos, 0, all_rows - 1)]
        visible = (
            (k_doc[None, :] == q_doc[:, None])
            & (k_pos[None, :] <= q_pos[:, None])
            & (k_pos >= 0)[None, :]
        )

        def compute(inner_state):
            running, totals, weighted = inner_state
            scores = (
                jnp.einsum("qhd,kd->hqk", query_rows, k_rows, preferred_element_type=jnp.float32)
                * score_scale
            )
            scores = jnp.where(visible[None], scores, -1e30)
            highest = jnp.maximum(running, jnp.max(scores, axis=2))
            rescale = jnp.exp(running - highest)
            weights = jnp.exp(scores - highest[:, :, None]) * visible[None].astype(jnp.float32)
            totals = rescale * totals + jnp.sum(weights, axis=2)
            weighted = weighted * jnp.transpose(rescale)[:, :, None] + jnp.einsum(
                "hqk,kd->qhd",
                weights.astype(jnp.bfloat16),
                v_rows,
                preferred_element_type=jnp.float32,
            )
            return (highest, totals, weighted)

        def keep(inner_state):
            return inner_state

        return lax.cond(jnp.any(visible), compute, keep, softmax_state)

    q_pos = my_group * tok_rows + jnp.arange(tok_rows, dtype=jnp.int32)
    query_rows = queries.reshape(tok_rows, heads_here, HD)
    q_doc = doc_all[q_pos]
    running = jnp.full((heads_here, tok_rows), -1e30, jnp.float32)
    totals = jnp.zeros((heads_here, tok_rows), jnp.float32)
    weighted = jnp.zeros((tok_rows, heads_here, HD), jnp.float32)
    k_rows, v_rows = sent_together((own_keys, own_values), DP, 0, 1)
    row_count = k_rows.shape[0]
    block_count = max(row_count // tok_rows, 1)
    block_rows = row_count // block_count

    def one_step(block_index, inner_state):
        k_block = lax.dynamic_slice_in_dim(k_rows, block_index * block_rows, block_rows, 0)
        v_block = lax.dynamic_slice_in_dim(v_rows, block_index * block_rows, block_rows, 0)
        return attend(
            inner_state, query_rows, q_pos, q_doc, k_block, v_block, block_index * block_rows
        )

    softmax_state = lax.fori_loop(0, block_count, one_step, (running, totals, weighted))
    running, totals, weighted = softmax_state
    home_rows = (
        (weighted / jnp.transpose(totals)[:, :, None])
        .reshape(tok_rows, q_width)
        .astype(jnp.bfloat16)
    )
    outgoing = home_rows.reshape(n_groups, piece_rows, q_width)[assignment[my_group]]
    attended = core_and_chips(outgoing, (("dp_0", "dp_1"), "dp_2"), (0, 1), 0, 0).reshape(
        tok_rows, q_width
    )
    return lax.psum_scatter(
        jnp.dot(attended, out_weight, preferred_element_type=jnp.float32).astype(jnp.bfloat16),
        "tensor",
        scatter_dimension=0,
        tiled=True,
    )


def solution(mesh):
    split = Mesh(
        mesh.devices.reshape(4, 4, 2, mesh.shape["tensor"]), ("dp_0", "dp_1", "dp_2", "tensor")
    )
    placed = (P(DP, "tensor"), P(DP, None), P(DP, None), P(), P(), P("tensor", None))
    return jax.shard_map(
        local, mesh=split, in_specs=placed, out_specs=P(DP_TENSOR, None), check_vma=False
    )
```

profile of v0, /device:TPU:6, one launch (start us, length us, event | category | flops | bytes accessed | tf_op | source)
XLA Modules:
  0.0 296.3 jit_solution(7686602018112683753)
XLA Ops:
  10.5 1.7 gather_fusion.1
  13.0 50.6 %all-gather.2.cloned.1.call-done = bf16[8192,256]{1,0:T(8,128)(2,1)} async-done(((bf16[256,256]{1,0:T(8,128)(2,1)}), bf16[8192,256]{1,0:T(8,128)(2,1)}) %all-gather.2.cloned.1.call-update) | async-done | bytes 4194320 | tf_op jit(solution)/shard_map/all_gather | solution.py:20
  63.5 3.8 %fusion.21 = (bf16[8192,128]{1,0:T(8,128)(2,1)S(1)}, bf16[8192,128]{1,0:T(8,128)(2,1)}) fusion(bf16[8192,256]{1,0:T(8,128)(2,1)} %all-gather.2.cloned.1.call-done), kind=kLoop, calls=%fused_computation.45 | loop fusion | bytes 8388608 | tf_op jit(solution)/shard_map/split | solution.py:20
  67.4 112.7 %while.18 = (s32[]{:T(128)}, f32[3,256]{1,0:T(4,128)S(1)}, f32[3,256]{1,0:T(4,128)S(1)}, f32[256,3,128]{2,0,1:T(8,128)S(1)}, s32[8192]{0:T(1024)S(1)}, /*index=5...) while((s32[]{:T(128)}, f32[3,256]{1,0:T(4,128)S(1)}, ...), condition=%wide.region_8.9_spmd.clone, body=%wide.region_2.8_spmd.clone.sunk | while | flops 103028224 | bytes 4523833 | solution.py:116
  67.5 1.7 gather_fusion
  70.9 1.7 gather_fusion
  74.3 1.7 gather_fusion
  77.7 1.7 gather_fusion
  81.1 1.7 gather_fusion
  84.5 1.7 gather_fusion
  87.8 1.8 conditional.3
  89.7 1.7 gather_fusion
  93.1 1.8 conditional.3
  95.0 1.7 gather_fusion
  98.4 1.7 gather_fusion
  101.8 1.7 gather_fusion
  105.2 1.7 gather_fusion
  108.6 1.7 gather_fusion
  112.0 1.7 gather_fusion
  115.4 1.7 gather_fusion
  118.8 1.7 gather_fusion
  122.2 1.7 gather_fusion
  125.7 1.7 gather_fusion
  129.1 1.7 gather_fusion
  132.5 1.7 gather_fusion
  135.9 1.7 gather_fusion
  139.3 1.7 gather_fusion
  142.7 1.7 gather_fusion
  181.3 51.3 %all_to_all.10 = bf16[16,2,1,8,384]{4,3,1,2,0:T(8,128)(2,1)S(1)} all-to-all(bf16[16,2,1,8,384]{4,3,1,2,0:T(8,128)(2,1)S(1)} %bitcast.40), channel_id=1, replica_groups=mesh['dp_0'=4,'dp_1'=4,'dp_2'=2,'tensor'=8] {'dp_0','dp_1'}, dimensions={0} | all-to-all | bytes 393216 | tf_op jit(solution)/shard_map/all_to_all | solution.py:38
  232.6 4.1 %all_to_all.11 = bf16[16,2,1,8,384]{4,3,0,2,1:T(8,128)(2,1)S(1)} all-to-all(bf16[16,2,1,8,384]{4,3,0,2,1:T(8,128)(2,1)S(1)} %copy.35), channel_id=1, replica_groups=mesh['dp_0'=4,'dp_1'=4,'dp_2'=2,'tensor'=8] {'dp_2'}, dimensions={1} | all-to-all | bytes 393216 | tf_op jit(solution)/shard_map/all_to_all | solution.py:38
  236.8 5.8 %convolution_convert_fusion = bf16[256,6144]{1,0:T(8,128)(2,1)} fusion(bf16[256,384]{1,0:T(8,128)(2,1)S(1)} %bitcast.43, bf16[384,6144]{1,0:T(8,128)(2,1)} %param.15), kind=kOutput, calls=%fused_computation.29 | convolution fusion | flops 1209532416 | bytes 8060928 | tf_op jit(solution)/shard_map/dot_general | solution.py:128
  242.7 46.9 %reduce-scatter.2.cloned.1.call-done = bf16[32,6144]{1,0:T(8,128)(2,1)} async-done(((bf16[256,6144]{1,0:T(8,128)(2,1)}), bf16[32,6144]{1,0:T(8,128)(2,1)}) %reduce-scatter.2.cloned.1.call-update) | async-done | bytes 393232 | tf_op jit(solution)/shard_map/reduce_scatter | solution.py:127
  (239 shorter events, 56.3 us)
Async XLA Ops:
  6.5 57.0 %all-gather.2.cloned.1.call-start = ((), (), s32[]{:S(2)}) async-start(), calls=%async_computation.3 | async-start | bytes 4325376 | tf_op jit(solution)/shard_map/all_gather | solution.py:20
  8.1 281.4 %reduce-scatter.2.cloned.1.call-start = ((), (), s32[]{:S(2)}) async-start(), calls=%async_computation.4 | async-start | bytes 3538944 | tf_op jit(solution)/shard_map/reduce_scatter | solution.py:127
Sparse Core Ops, SparseCore 0:
  9.9 53.6 all-gather.1
  242.8 46.6 reduce-scatter.1
where the time goes:
time: 297 us; the launch traced here: 296 us
  waiting for transfers between devices  97.5 us (33%)
  local copies, waits for them, and re-layouts  64.5 us (22%)
  blocking collectives  55.4 us (19%)
  other arithmetic  31.6 us (11%)
  loops' own time  24.8 us (8%)
  between operations  13.5 us (5%)
  matrix products  8.97 us (3%)
    all_to_all x2, blocking collectives, moved_by_axis(): result = lax.all_to_all(result, axes[k], k, k, tiled=True)  55.4 us
    gather x32, local copies, waits for them, and re-layouts, attend(): k_doc = doc_all[jnp.clip(k_pos, 0, all_rows - 1)]  55.1 us
    all_gather x1, waiting for transfers between devices, sent_together(): lax.all_gather(both, axis, axis=dim, tiled=True)  50.6 us
    reduce_scatter x1, waiting for transfers between devices, local(): lax.psum_scatter(jnp.dot(attended, out_weight, preferred_element_type=jnp...  46.9 us
    reduce_or x32, other arithmetic, attend(): return lax.cond(jnp.any(visible), compute, keep, softmax_state)  28.3 us
    another operation x1, loops' own time, local(): lax.fori_loop(0, block_count, one_step, (running, totals, weighted))  24.3 us
  transfers between devices with their start and end apart: 2, of which 2 were waited for; matrix products, arithmetic and copies ran while one was open for 2% of the time, Pallas kernels for 0%

commit v1 on v0

v1 whole, which is shorter than its diff:
```python
import functools

import jax
import jax.numpy as jnp
from jax import lax
from jax.experimental import pallas as pl
from jax.experimental.pallas import tpu as pltpu
from jax.sharding import Mesh
from jax.sharding import PartitionSpec as P

HD = 128
HEADS = 24
KV_HEADS = 4
DP = ("dp_0", "dp_1", "dp_2")
DP_TENSOR = ("dp_0", "dp_1", "dp_2", "tensor")
LOG2E = 1.4426950408889634
TILES = 4
BLOCK_K = 512
HIDDEN = -2e30
FLOOR = -1e30


def attention_kernel(
    group_ref, lengths_ref, assignment_ref, q_ref, kv_ref, o_ref, first_ref, last_ref, *, tok_rows
):
    rows = q_ref.shape[0]
    heads = q_ref.shape[1] // HD
    all_rows = kv_ref.shape[0]
    n_groups = assignment_ref.shape[0]
    piece = rows // n_groups
    tile = rows // TILES
    tile_pieces = n_groups // TILES
    factor = HD**-0.5 * LOG2E
    group = group_ref[0]

    ends, at = [], jnp.int32(0)
    for k in range(lengths_ref.shape[0]):
        at = at + lengths_ref[k]
        ends.append(at)

    def place(s):
        return s * tok_rows + assignment_ref[s, group] * piece

    def doc_start(position):
        start = jnp.zeros_like(position)
        for end in ends:
            start = jnp.where(position >= end, end, start)
        return start

    row = lax.broadcasted_iota(jnp.int32, (piece, HD), 0)
    lane = lax.broadcasted_iota(jnp.int32, (heads * tile, HD), 1)

    for t in range(TILES):
        for s in range(t * tile_pieces, (t + 1) * tile_pieces):
            position = place(s) + row
            last_ref[pl.ds(s * piece, piece), :] = position
            first_ref[pl.ds(s * piece, piece), :] = doc_start(position)

    for t in range(TILES):
        low = doc_start(place(t * tile_pieces))
        high = place((t + 1) * tile_pieces - 1) + piece
        low = low // 16 * 16
        count = (high - low + BLOCK_K - 1) // BLOCK_K
        low = jnp.minimum(low, all_rows - count * BLOCK_K)
        span = pl.ds(t * tile, tile)
        q = jnp.concatenate([q_ref[span, h * HD : (h + 1) * HD] for h in range(heads)], axis=0)
        first = jnp.concatenate([first_ref[span, :]] * heads, axis=0)
        last = jnp.concatenate([last_ref[span, :]] * heads, axis=0)

        def step(i, state):
            running, totals, weighted = state
            offset = pl.multiple_of(low + i * BLOCK_K, 16)
            k = kv_ref[pl.ds(offset, BLOCK_K), 0:HD]
            v = kv_ref[pl.ds(offset, BLOCK_K), HD : 2 * HD]
            scores = lax.dot_general(
                q, k, (((1,), (1,)), ((), ())), preferred_element_type=jnp.float32
            )
            parts = []
            for c in range(BLOCK_K // HD):
                position = lane + (offset + c * HD)
                visible = (position >= first) & (position <= last)
                parts.append(jnp.where(visible, scores[:, c * HD : (c + 1) * HD], HIDDEN))
            top = functools.reduce(jnp.maximum, parts)
            highest = jnp.maximum(running, jnp.max(top, axis=1, keepdims=True))
            rescale = jnp.exp2((running - highest) * factor)
            parts = [jnp.exp2((part - highest) * factor) for part in parts]
            totals = totals * rescale + functools.reduce(jnp.add, parts)
            weights = jnp.concatenate([part.astype(jnp.bfloat16) for part in parts], axis=1)
            weighted = weighted * rescale + jnp.dot(weights, v, preferred_element_type=jnp.float32)
            return highest, totals, weighted

        state = (
            jnp.full((heads * tile, 1), FLOOR, jnp.float32),
            jnp.zeros((heads * tile, HD), jnp.float32),
            jnp.zeros((heads * tile, HD), jnp.float32),
        )
        running, totals, weighted = lax.fori_loop(0, count, step, state)
        result = (weighted / jnp.sum(totals, axis=1, keepdims=True)).astype(o_ref.dtype)
        for h in range(heads):
            o_ref[span, h * HD : (h + 1) * HD] = result[h * tile : (h + 1) * tile]


def attention(group, lengths, assignment, q, kv, tok_rows):
    smem = pl.BlockSpec(memory_space=pltpu.SMEM)
    vmem = pl.BlockSpec(memory_space=pltpu.VMEM)
    return pl.pallas_call(
        functools.partial(attention_kernel, tok_rows=tok_rows),
        out_shape=jax.ShapeDtypeStruct(q.shape, q.dtype),
        in_specs=[smem, smem, smem, vmem, vmem],
        out_specs=vmem,
        scratch_shapes=[
            pltpu.VMEM((q.shape[0], HD), jnp.int32),
            pltpu.VMEM((q.shape[0], HD), jnp.int32),
        ],
        cost_estimate=pl.CostEstimate(
            flops=2 * 10**9, bytes_accessed=5 * 10**6, transcendentals=3 * 10**6
        ),
        name="attention",
    )(group, lengths, assignment, q, kv)


def local(queries, keys, values, lengths, assignment, out_weight):
    n_groups = lax.axis_size(DP)
    my_group = lax.axis_index(DP)
    my_lane = lax.axis_index("tensor")
    tok_rows, q_width = queries.shape
    piece = tok_rows // n_groups
    kv_head = my_lane * (q_width // HD) // (HEADS // KV_HEADS)
    own = jnp.concatenate(
        [lax.dynamic_slice_in_dim(a, kv_head * HD, HD, 1) for a in (keys, values)], axis=1
    )
    outgoing = queries.reshape(n_groups, piece, q_width)[assignment[my_group]]
    q = lax.all_to_all(outgoing, DP, 0, 0, tiled=True).reshape(tok_rows, q_width)
    kv = lax.all_gather(own, DP, axis=0, tiled=True)
    group = my_group.astype(jnp.int32).reshape(1)
    attended = attention(group, lengths, assignment, q, kv, tok_rows)
    return lax.psum_scatter(
        jnp.dot(attended, out_weight, preferred_element_type=jnp.float32).astype(jnp.bfloat16),
        "tensor",
        scatter_dimension=0,
        tiled=True,
    )


def solution(mesh):
    split = Mesh(
        mesh.devices.reshape(4, 4, 2, mesh.shape["tensor"]), ("dp_0", "dp_1", "dp_2", "tensor")
    )
    placed = (P(DP, "tensor"), P(DP, None), P(DP, None), P(), P(), P("tensor", None))
    return jax.shard_map(
        local, mesh=split, in_specs=placed, out_specs=P(DP_TENSOR, None), check_vma=False
    )
```

time: 297 us -> 140 us (0.47)
  local copies, waits for them, and re-layouts: 64.5 us -> 1.53 us
  blocking collectives: 55.4 us -> 14.1 us
  other arithmetic: 31.6 us -> 1.38 us
  loops' own time: 24.8 us -> 0 us
  Pallas kernels: 0 us -> 16.6 us
  waiting for transfers between devices: 97.5 us -> 86.9 us
  matrix products: 8.97 us -> 5.91 us
    gather x34 -> x1, local copies, waits for them, and re-layouts: 57.4 us -> 0.6 us  [local(): outgoing = queries.reshape(n_groups, piece, q_width)[assignment[my_group]]]
    all_to_all x2 -> x1, blocking collectives: 55.4 us -> 14.1 us  [local(): lax.all_to_all(outgoing, DP, 0, 0, tiled=True).reshape(tok_rows, q_width)]
    reduce_or x32 -> x0, other arithmetic: 28.3 us -> none  [attend(): return lax.cond(jnp.any(visible), compute, keep, softmax_state)]
    another operation x33 -> x0, loops' own time: 24.8 us -> none  [the longest x1 24.3 us: local(): lax.fori_loop(0, block_count, one_step, (running, totals, weighted))]
    pallas_call x0 -> x1, Pallas kernels: none -> 16.6 us  [attention(): pl.pallas_call(functools.partial(attention_kernel, tok_rows=tok_rows), ou...]
    all_gather x1, waiting for transfers between devices: 50.6 us -> 39.9 us  [local(): kv = lax.all_gather(own, DP, axis=0, tiled=True)]
    split x1 -> x0, local copies, waits for them, and re-layouts: 3.82 us -> none  [sent_together(): jnp.split(lax.all_gather(both, axis, axis=dim, tiled=True), ends, axis=al...]
    dot_general x4 -> x0, matrix products: 3.14 us -> none  [the longest x2 2.25 us: compute(): jnp.einsum('qhd,kd->hqk', query_rows, k_rows, preferred_element_type=jnp....]
  transfers between devices with their start and end apart: 2 -> 2, of which waited for: 2 -> 2; matrix products, arithmetic and copies ran while one was open for 2% -> 1% of each run, Pallas kernels for 0% -> 0%
where the time goes in v1:
time: 140 us
  waiting for transfers between devices  86.9 us (62%)
  Pallas kernels  16.6 us (12%)
  blocking collectives  14.1 us (10%)
  between operations  13.4 us (10%)
  matrix products  5.91 us (4%)
  local copies, waits for them, and re-layouts  1.53 us (1%)
    reduce_scatter x1, waiting for transfers between devices, local(): lax.psum_scatter(jnp.dot(attended, out_weight, preferred_element_type=jnp...  47 us
    all_gather x1, waiting for transfers between devices, local(): kv = lax.all_gather(own, DP, axis=0, tiled=True)  39.9 us
    pallas_call x1, Pallas kernels, attention(): pl.pallas_call(functools.partial(attention_kernel, tok_rows=tok_rows), ou...  16.6 us
    all_to_all x1, blocking collectives, local(): lax.all_to_all(outgoing, DP, 0, 0, tiled=True).reshape(tok_rows, q_width)  14.1 us
    dot_general x1, matrix products, local(): jnp.dot(attended, out_weight, preferred_element_type=jnp.float32)  5.91 us
  transfers between devices with their start and end apart: 2, of which 2 were waited for; matrix products, arithmetic and copies ran while one was open for 1% of the time, Pallas kernels for 0%

profile of v1, /device:TPU:6, one launch (start us, length us, event | category | flops | bytes accessed | tf_op | source)
XLA Modules:
  0.0 139.9 jit_solution(3064309971691484890)
XLA Ops:
  6.5 0.0 copy-start
  6.5 0.0 all-gather.2.cloned.1.call-start
  6.5 0.9 constant_dynamic-slice_fusion
  7.5 0.7 pad_maximum_fusion
  8.1 0.0 all-gather.2.cloned.1.call-update
  8.2 0.0 reduce-scatter.2.cloned.1.call-start
  8.2 0.7 fusion.1
  8.9 0.0 copy-done
  8.9 0.6 gather_fusion
  9.5 14.1 %all_to_all.5 = bf16[32,8,384]{2,1,0:T(8,128)(2,1)} all-to-all(bf16[32,8,384]{2,1,0:T(8,128)(2,1)S(1)} %gather_fusion), channel_id=1, replica_groups=mesh['dp_0'=4,'dp_1'=4,'dp_2'=2,'tensor'=8] {'dp_0','dp_1','dp_2'}, dimensions={0} | all-to-all | bytes 393216 | tf_op jit(solution)/shard_map/all_to_all | solution.py:133
  23.6 39.9 %all-gather.2.cloned.1.call-done.kv_ref = bf16[8192,256]{1,0:T(8,128)(2,1)} async-done(((bf16[256,256]{1,0:T(8,128)(2,1)}), bf16[8192,256]{1,0:T(8,128)(2,1)}) %all-gather.2.cloned.1.call-update) | async-done | bytes 4194320 | tf_op jit(solution)/shard_map/all_gather | solution.py:134
  63.5 16.6 %attention.1 = bf16[256,384]{1,0:T(8,128)(2,1)} custom-call(s32[1]{0:T(128)} %bitcast.group_ref, s32[16]{0:T(128)} %lengths_ref.1, s32[32,32]{1,0:T(8,128)} %assignment_ref.1, bf16[256,384]{1,0:T(8,128)(2,1)} %bitcast.14, bf16[8192,256]{1,0:T(8,128)(2,1)} %all-gather.2.cloned.1.call-done.kv_ref), custom_call_target="tpu_custom_call" | custom-call | flops 2000000000 | bytes 5000000 | tf_op jit(solution)/shard_map/attention/pallas_call | solution.py:106
  80.2 5.9 %convolution_convert_fusion = bf16[256,6144]{1,0:T(8,128)(2,1)} fusion(bf16[256,384]{1,0:T(8,128)(2,1)} %attention.1, bf16[384,6144]{1,0:T(8,128)(2,1)} %param.11), kind=kOutput, calls=%fused_computation.1 | convolution fusion | flops 1209532416 | bytes 8060928 | tf_op jit(solution)/shard_map/dot_general | solution.py:138
  86.1 0.0 reduce-scatter.2.cloned.1.call-update
  86.1 47.0 %reduce-scatter.2.cloned.1.call-done = bf16[32,6144]{1,0:T(8,128)(2,1)} async-done(((bf16[256,6144]{1,0:T(8,128)(2,1)}), bf16[32,6144]{1,0:T(8,128)(2,1)}) %reduce-scatter.2.cloned.1.call-update) | async-done | bytes 393232 | tf_op jit(solution)/shard_map/reduce_scatter | solution.py:137
  (1 shorter events, 0.0 us)
Async XLA Ops:
  6.5 2.4 %copy-start = (bf16[256,384]{1,0:T(8,128)(2,1)S(1)}, bf16[256,384]{1,0:T(8,128)(2,1)}, u32[]{:S(2)}) copy-start(bf16[256,384]{1,0:T(8,128)(2,1)} %param.6) | copy-start | bytes 589828
  6.5 57.0 %all-gather.2.cloned.1.call-start = ((), (), s32[]{:S(2)}) async-start(), calls=%async_computation.2 | async-start | bytes 4325376 | tf_op jit(solution)/shard_map/all_gather | solution.py:134
  8.2 124.9 %reduce-scatter.2.cloned.1.call-start = ((), (), s32[]{:S(2)}) async-start(), calls=%async_computation.3 | async-start | bytes 3538944 | tf_op jit(solution)/shard_map/reduce_scatter | solution.py:137
Sparse Core Ops, SparseCore 0:
  9.9 53.6 all-gather.1
  86.2 46.7 reduce-scatter.1

commit v2 on v1

v2 whole, which is shorter than its diff:
```python
import functools

import jax
import jax.numpy as jnp
from jax import lax
from jax.experimental import pallas as pl
from jax.experimental.pallas import tpu as pltpu
from jax.sharding import Mesh
from jax.sharding import PartitionSpec as P


HD = 128
HEADS = 24
KV_HEADS = 4
DP = ("dp_0", "dp_1", "dp_2")
DP_TENSOR = ("dp_0", "dp_1", "dp_2", "tensor")
LOG2E = 1.4426950408889634
BLOCK_K = 256
UNROLL = 4
COLUMNS = 512
HIDDEN = -2e30
FLOOR = -1e30


def attention_kernel(here_ref, lengths_ref, assignment_ref, q_ref, *refs, slots, lanes, tok_rows):
    sides = 4
    part_refs, weight_ref = refs[: 2 * sides], refs[2 * sides]
    out_refs = refs[2 * sides + 1 : 2 * sides + 1 + 2 * len(slots)]
    scratch = refs[2 * sides + 1 + 2 * len(slots) :]
    kv_ref, w_ref, qs_ref, first_ref, last_ref, scores_ref = scratch[:6]
    top_ref, totals_ref, weighted_ref, o_ref, tile_ref, offset_ref, kv_sem, w_sem = scratch[6:]
    rows = q_ref.shape[0]
    heads = q_ref.shape[1] // HD
    all_rows = kv_ref.shape[0]
    n_groups = assignment_ref.shape[0]
    piece = rows // n_groups
    chunk = rows // lanes
    pieces = n_groups // lanes
    half = tok_rows // 2
    n_tiles = len(slots)
    factor = HD**-0.5 * LOG2E
    y, x, core, my_lane = here_ref[0], here_ref[1], here_ref[2], here_ref[3]
    group = (y * sides + x) * 2 + core

    weight_copy = pltpu.make_async_copy(weight_ref, w_ref, w_sem)
    copies = []
    for swapped in range(2):
        holder = core if swapped == 0 else 1 - core
        along = jnp.where(holder == 0, x, y)
        across = jnp.where(holder == 0, y, x)
        for s in range(sides):
            for r in range(sides):
                u = lax.rem(along + sides - r, sides)
                v = lax.rem(across + sides - s, sides)
                py = jnp.where(holder == 0, v, u)
                px = jnp.where(holder == 0, u, v)
                for k in range(2):
                    source = (py * sides + px) * 2 + k
                    start = pl.multiple_of(source * tok_rows + holder * half, half)
                    begin = (r * 2 + k) * half
                    copies.append(
                        pltpu.make_async_copy(
                            part_refs[swapped * sides + s].at[pl.ds(begin, half), :],
                            kv_ref.at[pl.ds(start, half), :],
                            kv_sem.at[len(copies)],
                        )
                    )
    for copy in copies:
        copy.start()
    weight_copy.start()

    ends, at = [], jnp.int32(0)
    for k in range(lengths_ref.shape[0]):
        at = at + lengths_ref[k]
        ends.append(at)

    def place(s):
        return s * tok_rows + assignment_ref[s, group] * piece

    def doc_start(position):
        start = jnp.zeros_like(position)
        for end in ends:
            start = jnp.where(position >= end, end, start)
        return start

    row = lax.broadcasted_iota(jnp.int32, (piece, HD), 0)
    lane = lax.broadcasted_iota(jnp.int32, (heads * chunk, HD), 1)

    def fill(index, tile, offset):
        tile_ref[index] = tile
        offset_ref[index] = offset

    total = jnp.int32(0)
    for t, slot in enumerate(slots):
        owner = lax.rem(my_lane + slot, lanes)
        low = doc_start(place(owner * pieces)) // 16 * 16
        high = place(owner * pieces + pieces - 1) + piece
        count = (high - low + BLOCK_K - 1) // BLOCK_K
        low = jnp.minimum(low, all_rows - count * BLOCK_K)

        def add(i, carry, t=t, low=low, total=total):
            fill(total + i, t, low + i * BLOCK_K)
            return carry

        lax.fori_loop(0, count, add, 0)
        total = total + count
        begin = pl.multiple_of(owner * chunk, chunk)
        for h in range(heads):
            qs_ref[t, h * chunk : (h + 1) * chunk, :] = q_ref[
                pl.ds(begin, chunk), h * HD : (h + 1) * HD
            ]
        for p in range(pieces):
            position = place(owner * pieces + p) + row
            start = doc_start(position)
            for h in range(heads):
                span = pl.ds(h * chunk + p * piece, piece)
                last_ref[t, span, :] = position
                first_ref[t, span, :] = start
    for u in range(UNROLL - 1):
        fill(total + u, n_tiles, 0)
    steps = (total + UNROLL - 1) // UNROLL
    qs_ref[n_tiles] = jnp.zeros(qs_ref.shape[1:], qs_ref.dtype)
    first_ref[n_tiles] = jnp.ones(first_ref.shape[1:], jnp.int32)
    last_ref[n_tiles] = jnp.zeros(last_ref.shape[1:], jnp.int32)
    top_ref[...] = jnp.full(top_ref.shape, FLOOR, jnp.float32)
    totals_ref[...] = jnp.zeros(totals_ref.shape, jnp.float32)
    weighted_ref[...] = jnp.zeros(weighted_ref.shape, jnp.float32)
    for copy in copies:
        copy.wait()

    def score(i, carry):
        for u in range(UNROLL):
            index = i * UNROLL + u
            t = tile_ref[index]
            offset = pl.multiple_of(offset_ref[index], 16)
            scores = lax.dot_general(
                qs_ref[t],
                kv_ref[pl.ds(offset, BLOCK_K), 0:HD],
                (((1,), (1,)), ((), ())),
                preferred_element_type=jnp.float32,
            )
            first, last = first_ref[t], last_ref[t]
            parts = []
            for c in range(BLOCK_K // HD):
                position = lane + (offset + c * HD)
                visible = (position >= first) & (position <= last)
                part = jnp.where(visible, scores[:, c * HD : (c + 1) * HD], HIDDEN)
                scores_ref[index, :, c * HD : (c + 1) * HD] = part
                parts.append(part)
            top_ref[t] = jnp.maximum(top_ref[t], functools.reduce(jnp.maximum, parts))
        return carry

    lax.fori_loop(0, steps, score, 0)
    for t in range(n_tiles):
        top = top_ref[t]
        top_ref[t] = jnp.broadcast_to(jnp.max(top, axis=1, keepdims=True), top.shape)

    def weigh(i, carry):
        for u in range(UNROLL):
            index = i * UNROLL + u
            t = tile_ref[index]
            offset = pl.multiple_of(offset_ref[index], 16)
            top = top_ref[t]
            weights = [
                jnp.exp2((scores_ref[index, :, c * HD : (c + 1) * HD] - top) * factor)
                for c in range(BLOCK_K // HD)
            ]
            totals_ref[t] = totals_ref[t] + functools.reduce(jnp.add, weights)
            weights = jnp.concatenate([w.astype(jnp.bfloat16) for w in weights], axis=1)
            weighted_ref[t] = weighted_ref[t] + jnp.dot(
                weights,
                kv_ref[pl.ds(offset, BLOCK_K), HD : 2 * HD],
                preferred_element_type=jnp.float32,
            )
        return carry

    lax.fori_loop(0, steps, weigh, 0)
    for t in range(n_tiles):
        result = weighted_ref[t] / jnp.sum(totals_ref[t], axis=1, keepdims=True)
        for h in range(heads):
            o_ref[t * chunk : (t + 1) * chunk, h * HD : (h + 1) * HD] = result[
                h * chunk : (h + 1) * chunk
            ].astype(o_ref.dtype)
    weight_copy.wait()
    columns = out_refs[0].shape[1]
    width = COLUMNS
    for b in range(2 * columns // width):
        side, at = divmod(b * width, columns)
        share = jnp.dot(
            o_ref[...], w_ref[:, b * width : (b + 1) * width], preferred_element_type=jnp.float32
        ).astype(jnp.bfloat16)
        for t in range(n_tiles):
            out_refs[2 * t + side][:, at : at + width] = share[t * chunk : (t + 1) * chunk]


def attention(here, lengths, assignment, q, parts, out_weight, slots, tok_rows, lanes):
    smem = pl.BlockSpec(memory_space=pltpu.SMEM)
    vmem = pl.BlockSpec(memory_space=pltpu.VMEM)
    anywhere = pl.BlockSpec(memory_space=pl.ANY)
    all_rows = sum(part.shape[0] for part in parts)
    rows, q_width = q.shape
    chunk = rows // lanes
    stacked = q_width // HD * chunk
    n = len(slots)
    n_items = sum(min(4 * (d + 1), 28) + 1 for d in range(lanes))
    n_items = min(n_items, 29 * n) + UNROLL
    columns = out_weight.shape[1] // 2
    out = jax.ShapeDtypeStruct((chunk, columns), q.dtype)
    return pl.pallas_call(
        functools.partial(attention_kernel, slots=slots, lanes=lanes, tok_rows=tok_rows),
        out_shape=[out] * (2 * n),
        in_specs=[smem, smem, smem, vmem] + [anywhere] * (1 + len(parts)),
        out_specs=[vmem] * (2 * n),
        scratch_shapes=[
            pltpu.VMEM((all_rows, 2 * HD), q.dtype),
            pltpu.VMEM(out_weight.shape, q.dtype),
            pltpu.VMEM((n + 1, stacked, HD), q.dtype),
            pltpu.VMEM((n + 1, stacked, HD), jnp.int32),
            pltpu.VMEM((n + 1, stacked, HD), jnp.int32),
            pltpu.VMEM((n_items, stacked, BLOCK_K), jnp.float32),
            pltpu.VMEM((n + 1, stacked, HD), jnp.float32),
            pltpu.VMEM((n + 1, stacked, HD), jnp.float32),
            pltpu.VMEM((n + 1, stacked, HD), jnp.float32),
            pltpu.VMEM((n * chunk, q_width), q.dtype),
            pltpu.SMEM((n_items,), jnp.int32),
            pltpu.SMEM((n_items,), jnp.int32),
            pltpu.SemaphoreType.DMA((2 * all_rows // tok_rows,)),
            pltpu.SemaphoreType.DMA,
        ],
        cost_estimate=pl.CostEstimate(
            flops=2 * 10**9, bytes_accessed=10**7, transcendentals=2 * 10**6
        ),
        name="attention",
    )(here, lengths, assignment, q, *parts, out_weight)


def gathered(own, core):
    side = lax.axis_size("dp_0")
    half = own.shape[0] // 2

    def move(value, turn):
        pairs = []
        for y in range(side):
            for x in range(side):
                for c in range(2):
                    ty, tx, tc = turn(y, x, c)
                    target = (ty % side * side + tx % side) * 2 + tc
                    pairs.append(((y * side + x) * 2 + c, target))
        return lax.ppermute(value, DP, pairs)

    def swap(value):
        return move(value, lambda y, x, c: (y, x, 1 - c))

    def along(value, shift):
        return move(value, lambda y, x, c: (y, x + shift, c) if c == 0 else (y + shift, x, c))

    def across(value, shift):
        return move(value, lambda y, x, c: (y + shift, x, c) if c == 0 else (y, x + shift, c))

    keep = lax.dynamic_slice_in_dim(own, core * half, half, 0)
    other = swap(lax.dynamic_slice_in_dim(own, (1 - core) * half, half, 0))
    mine = jnp.where(
        core == 0,
        jnp.concatenate([keep, other], axis=0),
        jnp.concatenate([other, keep], axis=0),
    )
    row = jnp.concatenate([mine] + [along(mine, s) for s in (1, 2, 3)], axis=0)
    parts = [row] + [across(row, s) for s in (1, 2, 3)]
    return parts + [swap(part) for part in parts]


def scattered(shares, lanes):
    moving = {}
    for turn, h, j in hops(lanes):
        value = shares[j, h]
        if (turn, h) in moving:
            total = value.astype(jnp.float32) + moving[turn, h].astype(jnp.float32)
            value = total.astype(value.dtype)
        moving[turn, h] = lax.ppermute(
            value, "tensor", [(i, (i + turn) % lanes) for i in range(lanes)]
        )
    ends = []
    for h in range(2):
        total = shares[0, h].astype(jnp.float32)
        for turn in (1, -1):
            total = total + moving[turn, h].astype(jnp.float32)
        ends.append(total.astype(shares[0, h].dtype))
    return jnp.concatenate(ends, axis=1)


def hops(lanes):
    far = lanes // 2
    order = []
    for step in range(far):
        order += [(1, 0, far - step), (-1, 1, far + step)]
        if step < far - 1:
            order += [(1, 1, far - 1 - step), (-1, 0, far + 1 + step)]
    return order


def local(queries, keys, values, lengths, assignment, out_weight):
    n_groups = lax.axis_size(DP)
    lanes = lax.axis_size("tensor")
    my_group = lax.axis_index(DP)
    my_lane = lax.axis_index("tensor")
    core = lax.axis_index("dp_2")
    tok_rows, q_width = queries.shape
    piece = tok_rows // n_groups
    kv_head = my_lane * (q_width // HD) // (HEADS // KV_HEADS)
    own = jnp.concatenate(
        [lax.dynamic_slice_in_dim(a, kv_head * HD, HD, 1) for a in (keys, values)], axis=1
    )
    parts = gathered(own, core)
    outgoing = queries.reshape(n_groups, piece, q_width)[assignment[my_group]]
    q = lax.all_to_all(outgoing, DP, 0, 0, tiled=True)
    q = q.reshape(tok_rows, q_width)
    here = jnp.stack([lax.axis_index("dp_0"), lax.axis_index("dp_1"), core, my_lane])
    slots = (4, 3, 5, 2, 6, 1, 7, 0)
    outs = attention(
        here.astype(jnp.int32), lengths, assignment, q, parts, out_weight, slots, tok_rows, lanes
    )
    shares = {(slot, h): outs[2 * t + h] for t, slot in enumerate(slots) for h in range(2)}
    return scattered(shares, lanes)


def solution(mesh):
    lanes = mesh.shape["tensor"]
    split = Mesh(mesh.devices.reshape(4, 4, 2, lanes), DP_TENSOR)
    placed = (P(DP, "tensor"), P(DP, None), P(DP, None), P(), P(), P("tensor", None))

    return jax.shard_map(
        local, mesh=split, in_specs=placed, out_specs=P(DP_TENSOR, None), check_vma=False
    )
```

time: 140 us -> 114 us (0.81)
  the two profiles are of different devices: /device:TPU:6 before, /device:TPU:96 now
where the time goes in v2:
time: 114 us; the launch traced here: 113 us
  waiting for transfers between devices  41.8 us (37%)
  starting transfers between devices  37.4 us (33%)
  Pallas kernels  20.4 us (18%)
  other arithmetic  10.2 us (9%)
  local copies, waits for them, and re-layouts  3.19 us (3%)
    ppermute x14, starting transfers between devices, scattered(): lax.ppermute(value, 'tensor', [(i, (i + turn) % lanes) for i in range(lan...  23.7 us
    ppermute x11, waiting for transfers between devices, move(): return lax.ppermute(value, DP, pairs)  21.6 us
    pallas_call x1, Pallas kernels, attention(): pl.pallas_call(functools.partial(attention_kernel, slots=slots, lanes=lan...  20.4 us
    ppermute x14, waiting for transfers between devices, scattered(): lax.ppermute(value, 'tensor', [(i, (i + turn) % lanes) for i in range(lan...  12.6 us
    ppermute x11, starting transfers between devices, move(): return lax.ppermute(value, DP, pairs)  9.82 us
    convert_element_type x10, other arithmetic, scattered(): value = total.astype(value.dtype)  7.91 us
    all_to_all x1, waiting for transfers between devices, local(): q = lax.all_to_all(outgoing, DP, 0, 0, tiled=True)  7.55 us
    all_to_all x1, starting transfers between devices, local(): q = lax.all_to_all(outgoing, DP, 0, 0, tiled=True)  3.86 us
  transfers between devices with their start and end apart: 26, of which 10 were waited for; matrix products, arithmetic and copies ran while one was open for 9% of the time, Pallas kernels for 0%

profile of v2, /device:TPU:96, one launch (start us, length us, event | category | flops | bytes accessed | tf_op | source)
XLA Modules:
  0.0 113.3 jit_solution(5313635328511003094)
XLA Ops:
  0.0 0.9 constant_dynamic-slice_fusion
  1.1 1.2 %collective-permute-done = bf16[128,256]{1,0:T(8,128)(2,1)S(1)} collective-permute-done((bf16[128,256]{1,0:T(8,128)(2,1)S(1)}, bf16[128,256]{1,0:T(8,128)(2,1)S(1)}, u32[]{:S(2)}, u32[]{:S(2)}) %collective-permute-start) | collective-permute-done | bytes 65568 | tf_op jit(solution)/shard_map/ppermute | solution.py:249
  2.3 2.8 %collective-permute-start.3 = (bf16[256,256]{1,0:T(8,128)(2,1)S(1)}, bf16[256,256]{1,0:T(8,128)(2,1)S(1)}, u32[]{:S(2)}, u32[]{:S(2)}) collective-permute-start(bf16[256,256]{1,0:T(8,128)(2,1)S(1)} %maximum_select_fusion), channel_id=1, source_target_pairs={{0,48},{8,200},{16,0},{24,216},{32,16},{40,232},{48,32},{56,248},{... | collective-permute-start | bytes 393224 | tf_op jit(solution)/shard_map/ppermute | solution.py:249
  6.9 2.2 %collective-permute-done.3 = bf16[256,256]{1,0:T(8,128)(2,1)S(1)} collective-permute-done((bf16[256,256]{1,0:T(8,128)(2,1)S(1)}, bf16[256,256]{1,0:T(8,128)(2,1)S(1)}, u32[]{:S(2)}, u32[]{:S(2)}) %collective-permute-start.3) | collective-permute-done | bytes 131104 | tf_op jit(solution)/shard_map/ppermute | solution.py:249
  9.1 2.6 %collective-permute-done.2 = bf16[256,256]{1,0:T(8,128)(2,1)S(1)} collective-permute-done((bf16[256,256]{1,0:T(8,128)(2,1)S(1)}, bf16[256,256]{1,0:T(8,128)(2,1)S(1)}, u32[]{:S(2)}, u32[]{:S(2)}) %collective-permute-start.2) | collective-permute-done | bytes 131104 | tf_op jit(solution)/shard_map/ppermute | solution.py:249
  11.7 1.3 %collective-permute-done.1 = bf16[256,256]{1,0:T(8,128)(2,1)S(1)} collective-permute-done((bf16[256,256]{1,0:T(8,128)(2,1)S(1)}, bf16[256,256]{1,0:T(8,128)(2,1)S(1)}, u32[]{:S(2)}, u32[]{:S(2)}) %collective-permute-start.1) | collective-permute-done | bytes 131104 | tf_op jit(solution)/shard_map/ppermute | solution.py:249
  13.1 3.1 %collective-permute-start.6 = (bf16[1024,256]{1,0:T(8,128)(2,1)S(1)}, bf16[1024,256]{1,0:T(8,128)(2,1)S(1)}, u32[]{:S(2)}, u32[]{:S(2)}) collective-permute-start(bf16[1024,256]{1,0:T(8,128)(2,1)S(1)} %pad_maximum_fusion.refs_0_), channel_id=1, source_target_pairs={{0,192},{8,56},{16,208},{24,8},{32,224},{40,24},{48,240},{56,40},{... | collective-permute-start | bytes 1572872 | tf_op jit(solution)/shard_map/ppermute | solution.py:249
  16.8 1.0 collective-permute-start.4
  17.8 10.7 %collective-permute-done.6.refs_3_ = bf16[1024,256]{1,0:T(8,128)(2,1)S(1)} collective-permute-done((bf16[1024,256]{1,0:T(8,128)(2,1)S(1)}, bf16[1024,256]{1,0:T(8,128)(2,1)S(1)}, u32[]{:S(2)}, u32[]{:S(2)}) %collective-permute-start.6) | collective-permute-done | bytes 524320 | tf_op jit(solution)/shard_map/ppermute | solution.py:249
  29.0 3.5 %collective-permute-done.4.refs_1_ = bf16[1024,256]{1,0:T(8,128)(2,1)S(1)} collective-permute-done((bf16[1024,256]{1,0:T(8,128)(2,1)S(1)}, bf16[1024,256]{1,0:T(8,128)(2,1)S(1)}, u32[]{:S(2)}, u32[]{:S(2)}) %collective-permute-start.4) | collective-permute-done | bytes 524320 | tf_op jit(solution)/shard_map/ppermute | solution.py:249
  33.2 1.3 %gather_fusion = bf16[32,8,384]{2,1,0:T(8,128)(2,1)} fusion(bf16[32,8,384]{2,1,0:T(8,128)(2,1)S(1)} %bitcast.14, s32[1024]{0:T(1024)S(1)} %pad_clamp_fusion), kind=kCustom, calls=%fused_computation | custom fusion | bytes 393344 | tf_op jit(solution)/shard_map/gather | solution.py:314
  34.5 3.9 %all-to-all-start = ((bf16[32,8,384]{2,1,0:T(8,128)(2,1)}), bf16[32,8,384]{2,1,0:T(8,128)(2,1)S(1)}, u32[]{:S(2)}, u32[]{:S(2)}) async-start(bf16[32,8,384]{2,1,0:T(8,128)(2,1)} %gather_fusion), calls=%async_computation | async-start | bytes 393216 | tf_op jit(solution)/shard_map/all_to_all | solution.py:315
  39.0 7.5 %all-to-all-done = bf16[32,8,384]{2,1,0:T(8,128)(2,1)S(1)} async-done(((bf16[32,8,384]{2,1,0:T(8,128)(2,1)}), bf16[32,8,384]{2,1,0:T(8,128)(2,1)S(1)}, u32[]{:S(2)}, u32[]{:S(2)}) %all-to-all-start) | async-done | bytes 196640 | tf_op jit(solution)/shard_map/all_to_all | solution.py:315
  47.6 20.4 %attention.1 = (bf16[32,3072]{1,0:T(8,128)(2,1)}, bf16[32,3072]{1,0:T(8,128)(2,1)}, bf16[32,3072]{1,0:T(8,128)(2,1)}, bf16[32,3072]{1,0:T(8,128)(2,1)}, bf16[32,...) custom-call(s32[4]{0:T(128)} %pad_add_fusion.here_ref, ...), custom_call_target="tpu_custom_call" | custom-call | flops 2000000000 | bytes 10000000 | tf_op jit(solution)/shard_map/attention/pallas_call | solution.py:209
  68.0 3.2 %collective-permute-start.11 = (bf16[32,3072]{1,0:T(8,128)(2,1)}, bf16[32,3072]{1,0:T(8,128)(2,1)S(1)}, u32[]{:S(2)}, u32[]{:S(2)}) collective-permute-start(bf16[32,3072]{1,0:T(8,128)(2,1)} %get-tuple-element.25), channel_id=1, source_target_pairs={{0,1},{1,2},{2,3},{3,4},{4,5},{5,6},{6,7},{7,0},{8,9},{9,10},{10,1... | collective-permute-start | bytes 589832 | tf_op jit(solution)/shard_map/ppermute | solution.py:279
  71.2 3.2 %collective-permute-start.18 = (bf16[32,3072]{1,0:T(8,128)(2,1)}, bf16[32,3072]{1,0:T(8,128)(2,1)S(1)}, u32[]{:S(2)}, u32[]{:S(2)}) collective-permute-start(bf16[32,3072]{1,0:T(8,128)(2,1)} %get-tuple-element.32), channel_id=1, source_target_pairs={{0,1},{1,2},{2,3},{3,4},{4,5},{5,6},{6,7},{7,0},{8,9},{9,10},{10,1... | collective-permute-start | bytes 589832 | tf_op jit(solution)/shard_map/ppermute | solution.py:279
  74.5 2.4 %collective-permute-done.11 = bf16[32,3072]{1,0:T(8,128)(2,1)S(1)} collective-permute-done((bf16[32,3072]{1,0:T(8,128)(2,1)}, bf16[32,3072]{1,0:T(8,128)(2,1)S(1)}, u32[]{:S(2)}, u32[]{:S(2)}) %collective-permute-start.11) | collective-permute-done | bytes 196640 | tf_op jit(solution)/shard_map/ppermute | solution.py:279
  76.8 1.0 add_convert_fusion.11
  77.8 3.7 %collective-permute-start.12 = (bf16[32,3072]{1,0:T(8,128)(2,1)S(1)}, bf16[32,3072]{1,0:T(8,128)(2,1)S(1)}, u32[]{:S(2)}, u32[]{:S(2)}) collective-permute-start(bf16[32,3072]{1,0:T(8,128)(2,1)S(1)} %add_convert_fusion.11), channel_id=1, source_target_pairs={{0,1},{1,2},{2,3},{3,4},{4,5},{5,6},{6,7},{7,0},{8,9},{9,10},{10,1... | collective-permute-start | bytes 589832 | tf_op jit(solution)/shard_map/ppermute | solution.py:279
  81.5 1.0 add_convert_fusion.8
  82.5 1.0 add_convert_fusion.5
  83.5 3.3 %collective-permute-start.19 = (bf16[32,3072]{1,0:T(8,128)(2,1)S(1)}, bf16[32,3072]{1,0:T(8,128)(2,1)S(1)}, u32[]{:S(2)}, u32[]{:S(2)}) collective-permute-start(bf16[32,3072]{1,0:T(8,128)(2,1)S(1)} %add_convert_fusion.5), channel_id=1, source_target_pairs={{0,1},{1,2},{2,3},{3,4},{4,5},{5,6},{6,7},{7,0},{8,9},{9,10},{10,1... | collective-permute-start | bytes 589832 | tf_op jit(solution)/shard_map/ppermute | solution.py:279
  86.8 1.0 add_convert_fusion.3
  87.9 1.0 add_convert_fusion.10
  88.9 3.3 %collective-permute-start.13 = (bf16[32,3072]{1,0:T(8,128)(2,1)S(1)}, bf16[32,3072]{1,0:T(8,128)(2,1)S(1)}, u32[]{:S(2)}, u32[]{:S(2)}) collective-permute-start(bf16[32,3072]{1,0:T(8,128)(2,1)S(1)} %add_convert_fusion.10), channel_id=1, source_target_pairs={{0,1},{1,2},{2,3},{3,4},{4,5},{5,6},{6,7},{7,0},{8,9},{9,10},{10,1... | collective-permute-start | bytes 589832 | tf_op jit(solution)/shard_map/ppermute | solution.py:279
  92.2 1.0 add_convert_fusion.7
  93.3 1.0 add_convert_fusion.4
  94.2 3.3 %collective-permute-start.20 = (bf16[32,3072]{1,0:T(8,128)(2,1)S(1)}, bf16[32,3072]{1,0:T(8,128)(2,1)S(1)}, u32[]{:S(2)}, u32[]{:S(2)}) collective-permute-start(bf16[32,3072]{1,0:T(8,128)(2,1)S(1)} %add_convert_fusion.4), channel_id=1, source_target_pairs={{0,1},{1,2},{2,3},{3,4},{4,5},{5,6},{6,7},{7,0},{8,9},{9,10},{10,1... | collective-permute-start | bytes 589832 | tf_op jit(solution)/shard_map/ppermute | solution.py:279
  97.5 1.0 add_convert_fusion.2
  98.7 3.3 %collective-permute-start.14 = (bf16[32,3072]{1,0:T(8,128)(2,1)S(1)}, bf16[32,3072]{1,0:T(8,128)(2,1)S(1)}, u32[]{:S(2)}, u32[]{:S(2)}) collective-permute-start(bf16[32,3072]{1,0:T(8,128)(2,1)S(1)} %add_convert_fusion.9), channel_id=1, source_target_pairs={{0,1},{1,2},{2,3},{3,4},{4,5},{5,6},{6,7},{7,0},{8,9},{9,10},{10,1... | collective-permute-start | bytes 589832 | tf_op jit(solution)/shard_map/ppermute | solution.py:279
  102.0 3.5 %collective-permute-done.23 = bf16[32,3072]{1,0:T(8,128)(2,1)S(1)} collective-permute-done((bf16[32,3072]{1,0:T(8,128)(2,1)S(1)}, bf16[32,3072]{1,0:T(8,128)(2,1)S(1)}, u32[]{:S(2)}, u32[]{:S(2)}) %collective-permute-start.23) | collective-permute-done | bytes 196640 | tf_op jit(solution)/shard_map/ppermute | solution.py:279
  105.8 6.7 %collective-permute-done.24 = bf16[32,3072]{1,0:T(8,128)(2,1)S(1)} collective-permute-done((bf16[32,3072]{1,0:T(8,128)(2,1)S(1)}, bf16[32,3072]{1,0:T(8,128)(2,1)S(1)}, u32[]{:S(2)}, u32[]{:S(2)}) %collective-permute-start.24) | collective-permute-done | bytes 196640 | tf_op jit(solution)/shard_map/ppermute | solution.py:279
  (66 shorter events, 6.8 us)
Async XLA Ops:
  0.0 33.2 %copy-start = (bf16[256,384]{1,0:T(8,128)(2,1)S(1)}, bf16[256,384]{1,0:T(8,128)(2,1)}, u32[]{:S(2)}) copy-start(bf16[256,384]{1,0:T(8,128)(2,1)} %param.6) | copy-start | bytes 589828
  1.0 1.3 %collective-permute-start = (bf16[128,256]{1,0:T(8,128)(2,1)S(1)}, bf16[128,256]{1,0:T(8,128)(2,1)S(1)}, u32[]{:S(2)}, u32[]{:S(2)}) collective-permute-start(bf16[128,256]{1,0:T(8,128)(2,1)S(1)} %get-tuple-element.38), channel_id=1, source_target_pairs={{0,8},{8,0},{16,24},{24,16},{32,40},{40,32},{48,56},{56,48},{64,72... | collective-permute-start | bytes 196616 | tf_op jit(solution)/shard_map/ppermute | solution.py:249
  2.3 6.8 %collective-permute-start.3 = (bf16[256,256]{1,0:T(8,128)(2,1)S(1)}, bf16[256,256]{1,0:T(8,128)(2,1)S(1)}, u32[]{:S(2)}, u32[]{:S(2)}) collective-permute-start(bf16[256,256]{1,0:T(8,128)(2,1)S(1)} %maximum_select_fusion), channel_id=1, source_target_pairs={{0,48},{8,200},{16,0},{24,216},{32,16},{40,232},{48,32},{56,248},{... | collective-permute-start | bytes 393224 | tf_op jit(solution)/shard_map/ppermute | solution.py:249
  5.2 6.6 %collective-permute-start.2 = (bf16[256,256]{1,0:T(8,128)(2,1)S(1)}, bf16[256,256]{1,0:T(8,128)(2,1)S(1)}, u32[]{:S(2)}, u32[]{:S(2)}) collective-permute-start(bf16[256,256]{1,0:T(8,128)(2,1)S(1)} %maximum_select_fusion), channel_id=1, source_target_pairs={{0,32},{8,136},{16,48},{24,152},{32,0},{40,168},{48,16},{56,184},{... | collective-permute-start | bytes 393224 | tf_op jit(solution)/shard_map/ppermute | solution.py:249
  6.0 7.1 %collective-permute-start.1 = (bf16[256,256]{1,0:T(8,128)(2,1)S(1)}, bf16[256,256]{1,0:T(8,128)(2,1)S(1)}, u32[]{:S(2)}, u32[]{:S(2)}) collective-permute-start(bf16[256,256]{1,0:T(8,128)(2,1)S(1)} %maximum_select_fusion), channel_id=1, source_target_pairs={{0,16},{8,72},{16,32},{24,88},{32,48},{40,104},{48,0},{56,120},{64... | collective-permute-start | bytes 393224 | tf_op jit(solution)/shard_map/ppermute | solution.py:249
  13.1 33.5 %copy-start.1 = (bf16[1024,256]{1,0:T(8,128)(2,1)}, bf16[1024,256]{1,0:T(8,128)(2,1)S(1)}, u32[]{:S(2)}) copy-start(bf16[1024,256]{1,0:T(8,128)(2,1)S(1)} %pad_maximum_fusion.refs_0_) | copy-start | bytes 1572868
  13.1 15.4 %collective-permute-start.6 = (bf16[1024,256]{1,0:T(8,128)(2,1)S(1)}, bf16[1024,256]{1,0:T(8,128)(2,1)S(1)}, u32[]{:S(2)}, u32[]{:S(2)}) collective-permute-start(bf16[1024,256]{1,0:T(8,128)(2,1)S(1)} %pad_maximum_fusion.refs_0_), channel_id=1, source_target_pairs={{0,192},{8,56},{16,208},{24,8},{32,224},{40,24},{48,240},{56,40},{... | collective-permute-start | bytes 1572872 | tf_op jit(solution)/shard_map/ppermute | solution.py:249
  16.2 12.3 %collective-permute-start.5 = (bf16[1024,256]{1,0:T(8,128)(2,1)S(1)}, bf16[1024,256]{1,0:T(8,128)(2,1)S(1)}, u32[]{:S(2)}, u32[]{:S(2)}) collective-permute-start(bf16[1024,256]{1,0:T(8,128)(2,1)S(1)} %pad_maximum_fusion.refs_0_), channel_id=1, source_target_pairs={{0,128},{8,40},{16,144},{24,56},{32,160},{40,8},{48,176},{56,24},{... | collective-permute-start | bytes 1572872 | tf_op jit(solution)/shard_map/ppermute | solution.py:249
  16.8 15.7 %collective-permute-start.4 = (bf16[1024,256]{1,0:T(8,128)(2,1)S(1)}, bf16[1024,256]{1,0:T(8,128)(2,1)S(1)}, u32[]{:S(2)}, u32[]{:S(2)}) collective-permute-start(bf16[1024,256]{1,0:T(8,128)(2,1)S(1)} %pad_maximum_fusion.refs_0_), channel_id=1, source_target_pairs={{0,64},{8,24},{16,80},{24,40},{32,96},{40,56},{48,112},{56,8},{64,... | collective-permute-start | bytes 1572872 | tf_op jit(solution)/shard_map/ppermute | solution.py:249
  17.8 28.7 %collective-permute-start.7 = (bf16[1024,256]{1,0:T(8,128)(2,1)S(1)}, bf16[1024,256]{1,0:T(8,128)(2,1)S(1)}, u32[]{:S(2)}, u32[]{:S(2)}) collective-permute-start(bf16[1024,256]{1,0:T(8,128)(2,1)S(1)} %pad_maximum_fusion.refs_0_), channel_id=1, source_target_pairs={{0,8},{8,0},{16,24},{24,16},{32,40},{40,32},{48,56},{56,48},{64,72... | collective-permute-start | bytes 1572872 | tf_op jit(solution)/shard_map/ppermute | solution.py:249
  28.5 18.0 %collective-permute-start.10 = (bf16[1024,256]{1,0:T(8,128)(2,1)S(1)}, bf16[1024,256]{1,0:T(8,128)(2,1)S(1)}, u32[]{:S(2)}, u32[]{:S(2)}) collective-permute-start(bf16[1024,256]{1,0:T(8,128)(2,1)S(1)} %collective-permute-done.6.refs_3_), channel_id=1, source_target_pairs={{0,8},{8,0},{16,24},{24,16},{32,40},{40,32},{48,56},{56,48},{64,72... | collective-permute-start | bytes 1572872 | tf_op jit(solution)/shard_map/ppermute | solution.py:249
  28.5 18.0 %collective-permute-start.9 = (bf16[1024,256]{1,0:T(8,128)(2,1)S(1)}, bf16[1024,256]{1,0:T(8,128)(2,1)}, u32[]{:S(2)}, u32[]{:S(2)}) collective-permute-start(bf16[1024,256]{1,0:T(8,128)(2,1)S(1)} %collective-permute-done.5.refs_2_), channel_id=1, source_target_pairs={{0,8},{8,0},{16,24},{24,16},{32,40},{40,32},{48,56},{56,48},{64,72... | collective-permute-start | bytes 1572872 | tf_op jit(solution)/shard_map/ppermute | solution.py:249
  32.5 14.1 %collective-permute-start.8 = (bf16[1024,256]{1,0:T(8,128)(2,1)S(1)}, bf16[1024,256]{1,0:T(8,128)(2,1)}, u32[]{:S(2)}, u32[]{:S(2)}) collective-permute-start(bf16[1024,256]{1,0:T(8,128)(2,1)S(1)} %collective-permute-done.4.refs_1_), channel_id=1, source_target_pairs={{0,8},{8,0},{16,24},{24,16},{32,40},{40,32},{48,56},{56,48},{64,72... | collective-permute-start | bytes 1572872 | tf_op jit(solution)/shard_map/ppermute | solution.py:249
  34.5 12.0 %all-to-all-start = ((bf16[32,8,384]{2,1,0:T(8,128)(2,1)}), bf16[32,8,384]{2,1,0:T(8,128)(2,1)S(1)}, u32[]{:S(2)}, u32[]{:S(2)}) async-start(bf16[32,8,384]{2,1,0:T(8,128)(2,1)} %gather_fusion), calls=%async_computation | async-start | bytes 393216 | tf_op jit(solution)/shard_map/all_to_all | solution.py:315
  67.9 30.7 %copy-start.11 = (bf16[32,3072]{1,0:T(8,128)(2,1)S(1)}, bf16[32,3072]{1,0:T(8,128)(2,1)}, u32[]{:S(2)}) copy-start(bf16[32,3072]{1,0:T(8,128)(2,1)} %get-tuple-element.22) | copy-start | bytes 589828
  68.0 37.5 %copy-start.10 = (bf16[32,3072]{1,0:T(8,128)(2,1)S(1)}, bf16[32,3072]{1,0:T(8,128)(2,1)}, u32[]{:S(2)}) copy-start(bf16[32,3072]{1,0:T(8,128)(2,1)} %get-tuple-element.33) | copy-start | bytes 589828
  68.0 37.7 %copy-start.9 = (bf16[32,3072]{1,0:T(8,128)(2,1)S(1)}, bf16[32,3072]{1,0:T(8,128)(2,1)}, u32[]{:S(2)}) copy-start(bf16[32,3072]{1,0:T(8,128)(2,1)} %get-tuple-element.21) | copy-start | bytes 589828
  68.0 44.5 %copy-start.8 = (bf16[32,3072]{1,0:T(8,128)(2,1)S(1)}, bf16[32,3072]{1,0:T(8,128)(2,1)}, u32[]{:S(2)}) copy-start(bf16[32,3072]{1,0:T(8,128)(2,1)} %get-tuple-element.29) | copy-start | bytes 589828
  68.0 8.8 %collective-permute-start.11 = (bf16[32,3072]{1,0:T(8,128)(2,1)}, bf16[32,3072]{1,0:T(8,128)(2,1)S(1)}, u32[]{:S(2)}, u32[]{:S(2)}) collective-permute-start(bf16[32,3072]{1,0:T(8,128)(2,1)} %get-tuple-element.25), channel_id=1, source_target_pairs={{0,1},{1,2},{2,3},{3,4},{4,5},{5,6},{6,7},{7,0},{8,9},{9,10},{10,1... | collective-permute-start | bytes 589832 | tf_op jit(solution)/shard_map/ppermute | solution.py:279
  71.2 10.3 %collective-permute-start.15 = (bf16[32,3072]{1,0:T(8,128)(2,1)}, bf16[32,3072]{1,0:T(8,128)(2,1)S(1)}, u32[]{:S(2)}, u32[]{:S(2)}) collective-permute-start(bf16[32,3072]{1,0:T(8,128)(2,1)} %get-tuple-element.28), channel_id=1, source_target_pairs={{0,7},{1,0},{2,1},{3,2},{4,3},{5,4},{6,5},{7,6},{8,15},{9,8},{10,9... | collective-permute-start | bytes 589832 | tf_op jit(solution)/shard_map/ppermute | solution.py:279
  71.2 11.3 %collective-permute-start.18 = (bf16[32,3072]{1,0:T(8,128)(2,1)}, bf16[32,3072]{1,0:T(8,128)(2,1)S(1)}, u32[]{:S(2)}, u32[]{:S(2)}) collective-permute-start(bf16[32,3072]{1,0:T(8,128)(2,1)} %get-tuple-element.32), channel_id=1, source_target_pairs={{0,1},{1,2},{2,3},{3,4},{4,5},{5,6},{6,7},{7,0},{8,9},{9,10},{10,1... | collective-permute-start | bytes 589832 | tf_op jit(solution)/shard_map/ppermute | solution.py:279
  74.5 12.4 %collective-permute-start.21 = (bf16[32,3072]{1,0:T(8,128)(2,1)}, bf16[32,3072]{1,0:T(8,128)(2,1)S(1)}, u32[]{:S(2)}, u32[]{:S(2)}) collective-permute-start(bf16[32,3072]{1,0:T(8,128)(2,1)} %get-tuple-element.36), channel_id=1, source_target_pairs={{0,7},{1,0},{2,1},{3,2},{4,3},{5,4},{6,5},{7,6},{8,15},{9,8},{10,9... | collective-permute-start | bytes 589832 | tf_op jit(solution)/shard_map/ppermute | solution.py:279
  77.8 10.1 %collective-permute-start.12 = (bf16[32,3072]{1,0:T(8,128)(2,1)S(1)}, bf16[32,3072]{1,0:T(8,128)(2,1)S(1)}, u32[]{:S(2)}, u32[]{:S(2)}) collective-permute-start(bf16[32,3072]{1,0:T(8,128)(2,1)S(1)} %add_convert_fusion.11), channel_id=1, source_target_pairs={{0,1},{1,2},{2,3},{3,4},{4,5},{5,6},{6,7},{7,0},{8,9},{9,10},{10,1... | collective-permute-start | bytes 589832 | tf_op jit(solution)/shard_map/ppermute | solution.py:279
  82.4 9.7 %collective-permute-start.16 = (bf16[32,3072]{1,0:T(8,128)(2,1)S(1)}, bf16[32,3072]{1,0:T(8,128)(2,1)S(1)}, u32[]{:S(2)}, u32[]{:S(2)}) collective-permute-start(bf16[32,3072]{1,0:T(8,128)(2,1)S(1)} %add_convert_fusion.8), channel_id=1, source_target_pairs={{0,7},{1,0},{2,1},{3,2},{4,3},{5,4},{6,5},{7,6},{8,15},{9,8},{10,9... | collective-permute-start | bytes 589832 | tf_op jit(solution)/shard_map/ppermute | solution.py:279
  83.5 9.7 %collective-permute-start.19 = (bf16[32,3072]{1,0:T(8,128)(2,1)S(1)}, bf16[32,3072]{1,0:T(8,128)(2,1)S(1)}, u32[]{:S(2)}, u32[]{:S(2)}) collective-permute-start(bf16[32,3072]{1,0:T(8,128)(2,1)S(1)} %add_convert_fusion.5), channel_id=1, source_target_pairs={{0,1},{1,2},{2,3},{3,4},{4,5},{5,6},{6,7},{7,0},{8,9},{9,10},{10,1... | collective-permute-start | bytes 589832 | tf_op jit(solution)/shard_map/ppermute | solution.py:279
  87.8 9.7 %collective-permute-start.22 = (bf16[32,3072]{1,0:T(8,128)(2,1)S(1)}, bf16[32,3072]{1,0:T(8,128)(2,1)S(1)}, u32[]{:S(2)}, u32[]{:S(2)}) collective-permute-start(bf16[32,3072]{1,0:T(8,128)(2,1)S(1)} %add_convert_fusion.3), channel_id=1, source_target_pairs={{0,7},{1,0},{2,1},{3,2},{4,3},{5,4},{6,5},{7,6},{8,15},{9,8},{10,9... | collective-permute-start | bytes 589832 | tf_op jit(solution)/shard_map/ppermute | solution.py:279
  88.9 9.7 %collective-permute-start.13 = (bf16[32,3072]{1,0:T(8,128)(2,1)S(1)}, bf16[32,3072]{1,0:T(8,128)(2,1)S(1)}, u32[]{:S(2)}, u32[]{:S(2)}) collective-permute-start(bf16[32,3072]{1,0:T(8,128)(2,1)S(1)} %add_convert_fusion.10), channel_id=1, source_target_pairs={{0,1},{1,2},{2,3},{3,4},{4,5},{5,6},{6,7},{7,0},{8,9},{9,10},{10,1... | collective-permute-start | bytes 589832 | tf_op jit(solution)/shard_map/ppermute | solution.py:279
  93.2 12.5 %collective-permute-start.17 = (bf16[32,3072]{1,0:T(8,128)(2,1)S(1)}, bf16[32,3072]{1,0:T(8,128)(2,1)S(1)}, u32[]{:S(2)}, u32[]{:S(2)}) collective-permute-start(bf16[32,3072]{1,0:T(8,128)(2,1)S(1)} %add_convert_fusion.7), channel_id=1, source_target_pairs={{0,7},{1,0},{2,1},{3,2},{4,3},{5,4},{6,5},{7,6},{8,15},{9,8},{10,9... | collective-permute-start | bytes 589832 | tf_op jit(solution)/shard_map/ppermute | solution.py:279
  94.2 11.5 %collective-permute-start.20 = (bf16[32,3072]{1,0:T(8,128)(2,1)S(1)}, bf16[32,3072]{1,0:T(8,128)(2,1)S(1)}, u32[]{:S(2)}, u32[]{:S(2)}) collective-permute-start(bf16[32,3072]{1,0:T(8,128)(2,1)S(1)} %add_convert_fusion.4), channel_id=1, source_target_pairs={{0,1},{1,2},{2,3},{3,4},{4,5},{5,6},{6,7},{7,0},{8,9},{9,10},{10,1... | collective-permute-start | bytes 589832 | tf_op jit(solution)/shard_map/ppermute | solution.py:279
  98.5 7.0 %collective-permute-start.23 = (bf16[32,3072]{1,0:T(8,128)(2,1)S(1)}, bf16[32,3072]{1,0:T(8,128)(2,1)S(1)}, u32[]{:S(2)}, u32[]{:S(2)}) collective-permute-start(bf16[32,3072]{1,0:T(8,128)(2,1)S(1)} %add_convert_fusion.2), channel_id=1, source_target_pairs={{0,7},{1,0},{2,1},{3,2},{4,3},{5,4},{6,5},{7,6},{8,15},{9,8},{10,9... | collective-permute-start | bytes 589832 | tf_op jit(solution)/shard_map/ppermute | solution.py:279
  98.7 6.9 %collective-permute-start.14 = (bf16[32,3072]{1,0:T(8,128)(2,1)S(1)}, bf16[32,3072]{1,0:T(8,128)(2,1)S(1)}, u32[]{:S(2)}, u32[]{:S(2)}) collective-permute-start(bf16[32,3072]{1,0:T(8,128)(2,1)S(1)} %add_convert_fusion.9), channel_id=1, source_target_pairs={{0,1},{1,2},{2,3},{3,4},{4,5},{5,6},{6,7},{7,0},{8,9},{9,10},{10,1... | collective-permute-start | bytes 589832 | tf_op jit(solution)/shard_map/ppermute | solution.py:279
  105.5 7.0 %collective-permute-start.24 = (bf16[32,3072]{1,0:T(8,128)(2,1)S(1)}, bf16[32,3072]{1,0:T(8,128)(2,1)S(1)}, u32[]{:S(2)}, u32[]{:S(2)}) collective-permute-start(bf16[32,3072]{1,0:T(8,128)(2,1)S(1)} %add_convert_fusion.1), channel_id=1, source_target_pairs={{0,7},{1,0},{2,1},{3,2},{4,3},{5,4},{6,5},{7,6},{8,15},{9,8},{10,9... | collective-permute-start | bytes 589832 | tf_op jit(solution)/shard_map/ppermute | solution.py:279
  (6 other events, 52.8 us)

commit v3 on v2

--- a/solution.py
+++ b/solution.py
@@ -12,23 +12,30 @@
 HD = 128
 HEADS = 24
 KV_HEADS = 4
+MOST = 6144
 DP = ("dp_0", "dp_1", "dp_2")
 DP_TENSOR = ("dp_0", "dp_1", "dp_2", "tensor")
 LOG2E = 1.4426950408889634
-BLOCK_K = 256
-UNROLL = 4
+BLOCK_K = 512
+UNROLL = 12
 COLUMNS = 512
+VMEM_LIMIT = 60 * 1024 * 1024
 HIDDEN = -2e30
 FLOOR = -1e30
 
-
-def attention_kernel(here_ref, lengths_ref, assignment_ref, q_ref, *refs, slots, lanes, tok_rows):
+HELD = ((0, (0, 1, 2, 3)), (1, (0, 1, 2, 3)), (3, (0, 1, 2, 3)), (2, (0, 1)), (2, (2, 3)))
+
+
+def attention_kernel(here_ref, lengths_ref, assignment_ref, q_ref, *refs, layout, lanes, tok_rows):
     sides = 4
-    part_refs, weight_ref = refs[: 2 * sides], refs[2 * sides]
-    out_refs = refs[2 * sides + 1 : 2 * sides + 1 + 2 * len(slots)]
-    scratch = refs[2 * sides + 1 + 2 * len(slots) :]
-    kv_ref, w_ref, qs_ref, first_ref, last_ref, scores_ref = scratch[:6]
-    top_ref, totals_ref, weighted_ref, o_ref, tile_ref, offset_ref, kv_sem, w_sem = scratch[6:]
+    n_parts = 2 * len(HELD)
+    part_refs, weight_ref = refs[:n_parts], refs[n_parts]
+    out_refs = refs[n_parts + 1 : n_parts + 1 + len(layout)]
+    scratch = refs[n_parts + 1 + len(layout) :]
+    slots = range(lanes)
+    kv_ref, w_ref, qs_ref, behind_ref, reach_ref, scores_ref = scratch[:6]
+    top_ref, totals_ref, weighted_ref, o_ref, share_ref, tile_ref, offset_ref = scratch[6:13]
+    kv_sem, w_sem, out_sem = scratch[13:]
     rows = q_ref.shape[0]
     heads = q_ref.shape[1] // HD
     all_rows = kv_ref.shape[0]
@@ -36,7 +43,6 @@
     piece = rows // n_groups
     chunk = rows // lanes
     pieces = n_groups // lanes
-    half = tok_rows // 2
     n_tiles = len(slots)
     factor = HD**-0.5 * LOG2E
     y, x, core, my_lane = here_ref[0], here_ref[1], here_ref[2], here_ref[3]
@@ -48,26 +54,23 @@
         holder = core if swapped == 0 else 1 - core
         along = jnp.where(holder == 0, x, y)
         across = jnp.where(holder == 0, y, x)
-        for s in range(sides):
-            for r in range(sides):
+        for n, (s, blocks) in enumerate(HELD):
+            for b, r in enumerate(blocks):
                 u = lax.rem(along + sides - r, sides)
                 v = lax.rem(across + sides - s, sides)
                 py = jnp.where(holder == 0, v, u)
                 px = jnp.where(holder == 0, u, v)
-                for k in range(2):
-                    source = (py * sides + px) * 2 + k
-                    start = pl.multiple_of(source * tok_rows + holder * half, half)
-                    begin = (r * 2 + k) * half
-                    copies.append(
-                        pltpu.make_async_copy(
-                            part_refs[swapped * sides + s].at[pl.ds(begin, half), :],
-                            kv_ref.at[pl.ds(start, half), :],
-                            kv_sem.at[len(copies)],
-                        )
+                source = (py * sides + px) * 2 + holder
+                start = pl.multiple_of(source * tok_rows, tok_rows)
+                copies.append(
+                    pltpu.make_async_copy(
+                        part_refs[swapped * len(HELD) + n].at[pl.ds(b * tok_rows, tok_rows), :],
+                        kv_ref.at[pl.ds(start, tok_rows), :],
+                        kv_sem.at[len(copies)],
                     )
+                )
     for copy in copies:
         copy.start()
-    weight_copy.start()
 
     ends, at = [], jnp.int32(0)
     for k in range(lengths_ref.shape[0]):
@@ -84,7 +87,7 @@
         return start
 
     row = lax.broadcasted_iota(jnp.int32, (piece, HD), 0)
-    lane = lax.broadcasted_iota(jnp.int32, (heads * chunk, HD), 1)
+    lane = lax.broadcasted_iota(jnp.int32, (piece, HD), 1)
 
     def fill(index, tile, offset):
         tile_ref[index] = tile
@@ -114,19 +117,20 @@
             start = doc_start(position)
             for h in range(heads):
                 span = pl.ds(h * chunk + p * piece, piece)
-                last_ref[t, span, :] = position
-                first_ref[t, span, :] = start
+                behind_ref[t, span, :] = (lane - start).astype(jnp.uint32)
+                reach_ref[t, span, :] = (position - start).astype(jnp.uint32)
     for u in range(UNROLL - 1):
         fill(total + u, n_tiles, 0)
     steps = (total + UNROLL - 1) // UNROLL
     qs_ref[n_tiles] = jnp.zeros(qs_ref.shape[1:], qs_ref.dtype)
-    first_ref[n_tiles] = jnp.ones(first_ref.shape[1:], jnp.int32)
-    last_ref[n_tiles] = jnp.zeros(last_ref.shape[1:], jnp.int32)
+    behind_ref[n_tiles] = jnp.zeros(behind_ref.shape[1:], jnp.uint32)
+    reach_ref[n_tiles] = jnp.zeros(reach_ref.shape[1:], jnp.uint32)
     top_ref[...] = jnp.full(top_ref.shape, FLOOR, jnp.float32)
     totals_ref[...] = jnp.zeros(totals_ref.shape, jnp.float32)
     weighted_ref[...] = jnp.zeros(weighted_ref.shape, jnp.float32)
     for copy in copies:
         copy.wait()
+    weight_copy.start()
 
     def score(i, carry):
         for u in range(UNROLL):
@@ -139,11 +143,10 @@
                 (((1,), (1,)), ((), ())),
                 preferred_element_type=jnp.float32,
             )
-            first, last = first_ref[t], last_ref[t]
+            behind, reach = behind_ref[t], reach_ref[t]
             parts = []
             for c in range(BLOCK_K // HD):
-                position = lane + (offset + c * HD)
-                visible = (position >= first) & (position <= last)
+                visible = behind + (offset + c * HD).astype(jnp.uint32) <= reach
                 part = jnp.where(visible, scores[:, c * HD : (c + 1) * HD], HIDDEN)
                 scores_ref[index, :, c * HD : (c + 1) * HD] = part
                 parts.append(part)
@@ -184,59 +187,76 @@
     weight_copy.wait()
     columns = out_refs[0].shape[1]
     width = COLUMNS
+
+    leaving = {}
+    for out_ref, held in zip(out_refs, layout):
+        for n, (slot, side) in enumerate(held):
+            leaving[slot, side] = pltpu.make_async_copy(
+                share_ref.at[2 * slot + side],
+                out_ref.at[pl.ds(n * chunk, chunk), :],
+                out_sem.at[2 * slot + side],
+            )
+
     for b in range(2 * columns // width):
         side, at = divmod(b * width, columns)
         share = jnp.dot(
             o_ref[...], w_ref[:, b * width : (b + 1) * width], preferred_element_type=jnp.float32
         ).astype(jnp.bfloat16)
         for t in range(n_tiles):
-            out_refs[2 * t + side][:, at : at + width] = share[t * chunk : (t + 1) * chunk]
-
-
-def attention(here, lengths, assignment, q, parts, out_weight, slots, tok_rows, lanes):
+            share_ref[2 * t + side, :, at : at + width] = share[t * chunk : (t + 1) * chunk]
+        if at + width == columns:
+            for t in range(n_tiles):
+                leaving[t, side].start()
+    for copy in leaving.values():
+        copy.wait()
+
+
+def attention(here, lengths, assignment, q, parts, out_weight, layout, tok_rows, lanes):
     smem = pl.BlockSpec(memory_space=pltpu.SMEM)
     vmem = pl.BlockSpec(memory_space=pltpu.VMEM)
-    anywhere = pl.BlockSpec(memory_space=pl.ANY)
+    hbm = pl.BlockSpec(memory_space=pltpu.HBM)
     all_rows = sum(part.shape[0] for part in parts)
     rows, q_width = q.shape
     chunk = rows // lanes
     stacked = q_width // HD * chunk
-    n = len(slots)
-    n_items = sum(min(4 * (d + 1), 28) + 1 for d in range(lanes))
-    n_items = min(n_items, 29 * n) + UNROLL
+    n = lanes
+    blocks = [pl.cdiv(min((d + 1) * rows * 4, MOST + rows * 4) + 15, BLOCK_K) for d in range(lanes)]
+    n_items = sum(blocks) + UNROLL
     columns = out_weight.shape[1] // 2
-    out = jax.ShapeDtypeStruct((chunk, columns), q.dtype)
+    outs = [jax.ShapeDtypeStruct((chunk * len(held), columns), q.dtype) for held in layout]
     return pl.pallas_call(
-        functools.partial(attention_kernel, slots=slots, lanes=lanes, tok_rows=tok_rows),
-        out_shape=[out] * (2 * n),
-        in_specs=[smem, smem, smem, vmem] + [anywhere] * (1 + len(parts)),
-        out_specs=[vmem] * (2 * n),
+        functools.partial(attention_kernel, layout=layout, lanes=lanes, tok_rows=tok_rows),
+        out_shape=outs,
+        in_specs=[smem, smem, smem, vmem] + [hbm] * (1 + len(parts)),
+        out_specs=[hbm] * len(outs),
         scratch_shapes=[
             pltpu.VMEM((all_rows, 2 * HD), q.dtype),
             pltpu.VMEM(out_weight.shape, q.dtype),
             pltpu.VMEM((n + 1, stacked, HD), q.dtype),
-            pltpu.VMEM((n + 1, stacked, HD), jnp.int32),
-            pltpu.VMEM((n + 1, stacked, HD), jnp.int32),
+            pltpu.VMEM((n + 1, stacked, HD), jnp.uint32),
+            pltpu.VMEM((n + 1, stacked, HD), jnp.uint32),
             pltpu.VMEM((n_items, stacked, BLOCK_K), jnp.float32),
             pltpu.VMEM((n + 1, stacked, HD), jnp.float32),
             pltpu.VMEM((n + 1, stacked, HD), jnp.float32),
             pltpu.VMEM((n + 1, stacked, HD), jnp.float32),
             pltpu.VMEM((n * chunk, q_width), q.dtype),
+            pltpu.VMEM((2 * n, chunk, columns), q.dtype),
             pltpu.SMEM((n_items,), jnp.int32),
             pltpu.SMEM((n_items,), jnp.int32),
-            pltpu.SemaphoreType.DMA((2 * all_rows // tok_rows,)),
+            pltpu.SemaphoreType.DMA((all_rows // tok_rows,)),
             pltpu.SemaphoreType.DMA,
+            pltpu.SemaphoreType.DMA((2 * n,)),
         ],
         cost_estimate=pl.CostEstimate(
             flops=2 * 10**9, bytes_accessed=10**7, transcendentals=2 * 10**6
         ),
+        compiler_params=pltpu.CompilerParams(vmem_limit_bytes=VMEM_LIMIT),
         name="attention",
     )(here, lengths, assignment, q, *parts, out_weight)
 
 
-def gathered(own, core):
+def gathered(own, *between):
     side = lax.axis_size("dp_0")
-    half = own.shape[0] // 2
 
     def move(value, turn):
         pairs = []
@@ -257,19 +277,22 @@
     def across(value, shift):
         return move(value, lambda y, x, c: (y + shift, x, c) if c == 0 else (y, x + shift, c))
 
-    keep = lax.dynamic_slice_in_dim(own, core * half, half, 0)
-    other = swap(lax.dynamic_slice_in_dim(own, (1 - core) * half, half, 0))
-    mine = jnp.where(
-        core == 0,
-        jnp.concatenate([keep, other], axis=0),
-        jnp.concatenate([other, keep], axis=0),
-    )
-    row = jnp.concatenate([mine] + [along(mine, s) for s in (1, 2, 3)], axis=0)
-    parts = [row] + [across(row, s) for s in (1, 2, 3)]
-    return parts + [swap(part) for part in parts]
-
-
-def scattered(shares, lanes):
+    row = [own] + [along(own, s) for s in (1, 2, 3)]
+    row, between = lax.optimization_barrier((row, between))
+    row = jnp.concatenate(row, axis=0)
+    half = row.shape[0] // 2
+    back, front = across(row, 1), across(row, 3)
+    ahead = [across(back[:half], 1), across(front[half:], 3)]
+    parts = [row, back, front] + ahead
+    return parts + [swap(part) for part in parts], *between
+
+
+def scattered(outs, layout, lanes):
+    chunk = outs[0].shape[0]
+    shares = {}
+    for out, held in zip(outs, layout):
+        for n, (slot, h) in enumerate(held):
+            shares[slot, h] = out[n * chunk : (n + 1) * chunk]
     moving = {}
     for turn, h, j in hops(lanes):
         value = shares[j, h]
@@ -279,13 +302,16 @@
         moving[turn, h] = lax.ppermute(
             value, "tensor", [(i, (i + turn) % lanes) for i in range(lanes)]
         )
-    ends = []
-    for h in range(2):
-        total = shares[0, h].astype(jnp.float32)
-        for turn in (1, -1):
-            total = total + moving[turn, h].astype(jnp.float32)
-        ends.append(total.astype(shares[0, h].dtype))
-    return jnp.concatenate(ends, axis=1)
+    terms = [[shares[0, h] for h in range(2)]]
+    terms += [[moving[turn, h] for h in range(2)] for turn in (1, -1)]
+    total = sum(jnp.concatenate(term, axis=1).astype(jnp.float32) for term in terms)
+    return total.astype(outs[0].dtype)
+
+
+def handed(lanes):
+    order = [(j, h) for _, h, j in hops(lanes)]
+    pairs = [tuple(order[n : n + 2]) for n in range(4, len(order), 2)]
+    return tuple((one,) for one in order[:4]) + tuple(pairs) + (((0, 0),), ((0, 1),))
 
 
 def hops(lanes):
@@ -310,17 +336,14 @@
     own = jnp.concatenate(
         [lax.dynamic_slice_in_dim(a, kv_head * HD, HD, 1) for a in (keys, values)], axis=1
     )
-    parts = gathered(own, core)
     outgoing = queries.reshape(n_groups, piece, q_width)[assignment[my_group]]
+    here = jnp.stack([lax.axis_index("dp_0"), lax.axis_index("dp_1"), core, my_lane])
+    parts, outgoing, here = gathered(own, outgoing, here.astype(jnp.int32))
     q = lax.all_to_all(outgoing, DP, 0, 0, tiled=True)
     q = q.reshape(tok_rows, q_width)
-    here = jnp.stack([lax.axis_index("dp_0"), lax.axis_index("dp_1"), core, my_lane])
-    slots = (4, 3, 5, 2, 6, 1, 7, 0)
-    outs = attention(
-        here.astype(jnp.int32), lengths, assignment, q, parts, out_weight, slots, tok_rows, lanes
-    )
-    shares = {(slot, h): outs[2 * t + h] for t, slot in enumerate(slots) for h in range(2)}
-    return scattered(shares, lanes)
+    layout = handed(lanes)
+    outs = attention(here, lengths, assignment, q, parts, out_weight, layout, tok_rows, lanes)
+    return scattered(outs, layout, lanes)
 
 
 def solution(mesh):

time: 114 us -> 102 us (0.89)
  the two profiles are of different devices: /device:TPU:96 before, /device:TPU:6 now
where the time goes in v3:
time: 102 us
  starting transfers between devices  34.2 us (34%)
  waiting for transfers between devices  30.7 us (30%)
  Pallas kernels  13.9 us (14%)
  blocking collectives  12.7 us (12%)
  other arithmetic  6.85 us (7%)
  local copies, waits for them, and re-layouts  3.11 us (3%)
    ppermute x14, starting transfers between devices, scattered(): lax.ppermute(value, 'tensor', [(i, (i + turn) % lanes) for i in range(lan...  22.3 us
    ppermute x12, waiting for transfers between devices, move(): return lax.ppermute(value, DP, pairs)  16.4 us
    ppermute x14, waiting for transfers between devices, scattered(): lax.ppermute(value, 'tensor', [(i, (i + turn) % lanes) for i in range(lan...  14.3 us
    pallas_call x1, Pallas kernels, attention(): pl.pallas_call(functools.partial(attention_kernel, layout=layout, lanes=l...  13.9 us
    all_to_all x1, blocking collectives, local(): q = lax.all_to_all(outgoing, DP, 0, 0, tiled=True)  12.7 us
    ppermute x12, starting transfers between devices, move(): return lax.ppermute(value, DP, pairs)  11.9 us
    convert_element_type x5, other arithmetic, scattered(): value = total.astype(value.dtype)  4.59 us
  transfers between devices with their start and end apart: 26, of which 15 were waited for; matrix products, arithmetic and copies ran while one was open for 6% of the time, Pallas kernels for 0%

profile of v3, /device:TPU:6, one launch (start us, length us, event | category | flops | bytes accessed | tf_op | source)
XLA Modules:
  0.0 101.6 jit_solution(3223121495254142318)
XLA Ops:
  0.0 0.9 constant_dynamic-slice_fusion.1
  1.0 0.9 collective-permute-start.2
  1.9 2.8 %collective-permute-start.1 = (bf16[256,256]{1,0:T(8,128)(2,1)S(1)}, bf16[256,256]{1,0:T(8,128)(2,1)S(1)}, u32[]{:S(2)}, u32[]{:S(2)}) collective-permute-start(bf16[256,256]{1,0:T(8,128)(2,1)S(1)} %pad_maximum_fusion), channel_id=1, source_target_pairs={{0,32},{8,136},{16,48},{24,152},{32,0},{40,168},{48,16},{56,184},{... | collective-permute-start | bytes 393224 | tf_op jit(solution)/shard_map/ppermute | solution.py:269
  7.2 1.8 %collective-permute-done.1 = bf16[256,256]{1,0:T(8,128)(2,1)S(1)} collective-permute-done((bf16[256,256]{1,0:T(8,128)(2,1)S(1)}, bf16[256,256]{1,0:T(8,128)(2,1)S(1)}, u32[]{:S(2)}, u32[]{:S(2)}) %collective-permute-start.1) | collective-permute-done | bytes 131104 | tf_op jit(solution)/shard_map/ppermute | solution.py:269
  9.7 2.9 %collective-permute-start.4 = (bf16[1024,256]{1,0:T(8,128)(2,1)S(1)}, bf16[1024,256]{1,0:T(8,128)(2,1)S(1)}, u32[]{:S(2)}, u32[]{:S(2)}) collective-permute-start(bf16[1024,256]{1,0:T(8,128)(2,1)S(1)} %constant_dynamic-update-slice_fusion.refs_0_), channel_id=1, source_target_pairs={{0,192},{8,56},{16,208},{24,8},{32,224},{40,24},{48,240},{56,40},{... | collective-permute-start | bytes 1572872 | tf_op jit(solution)/shard_map/ppermute | solution.py:269
  13.2 6.2 %collective-permute-done.4.refs_2_ = bf16[1024,256]{1,0:T(8,128)(2,1)S(1)} collective-permute-done((bf16[1024,256]{1,0:T(8,128)(2,1)S(1)}, bf16[1024,256]{1,0:T(8,128)(2,1)S(1)}, u32[]{:S(2)}, u32[]{:S(2)}) %collective-permute-start.4) | collective-permute-done | bytes 524320 | tf_op jit(solution)/shard_map/ppermute | solution.py:269
  19.4 3.8 %collective-permute-start.6 = (bf16[512,256]{1,0:T(8,128)(2,1)S(1)}, bf16[512,256]{1,0:T(8,128)(2,1)S(1)}, u32[]{:S(2)}, u32[]{:S(2)}) collective-permute-start(bf16[512,256]{1,0:T(8,128)(2,1)S(1)} %slice.51), channel_id=1, source_target_pairs={{0,192},{8,56},{16,208},{24,8},{32,224},{40,24},{48,240},{56,40},{... | collective-permute-start | bytes 786440 | tf_op jit(solution)/shard_map/ppermute | solution.py:269
  23.8 3.3 %collective-permute-done.6.refs_4_ = bf16[512,256]{1,0:T(8,128)(2,1)S(1)} collective-permute-done((bf16[512,256]{1,0:T(8,128)(2,1)S(1)}, bf16[512,256]{1,0:T(8,128)(2,1)S(1)}, u32[]{:S(2)}, u32[]{:S(2)}) %collective-permute-start.6) | collective-permute-done | bytes 262176 | tf_op jit(solution)/shard_map/ppermute | solution.py:269
  27.0 4.3 %collective-permute-done.5.refs_3_ = bf16[512,256]{1,0:T(8,128)(2,1)S(1)} collective-permute-done((bf16[512,256]{1,0:T(8,128)(2,1)S(1)}, bf16[512,256]{1,0:T(8,128)(2,1)S(1)}, u32[]{:S(2)}, u32[]{:S(2)}) %collective-permute-start.5) | collective-permute-done | bytes 262176 | tf_op jit(solution)/shard_map/ppermute | solution.py:269
  31.4 12.7 %all_to_all.5 = bf16[32,8,384]{2,1,0:T(8,128)(2,1)} all-to-all(bf16[32,8,384]{2,1,0:T(8,128)(2,1)S(1)} %gather_fusion), channel_id=1, replica_groups=mesh['dp_0'=4,'dp_1'=4,'dp_2'=2,'tensor'=8] {'dp_0','dp_1','dp_2'}, dimensions={0} | all-to-all | bytes 393216 | tf_op jit(solution)/shard_map/all_to_all | solution.py:342
  45.6 13.9 %attention.1 = (bf16[32,3072]{1,0:T(8,128)(2,1)}, bf16[32,3072]{1,0:T(8,128)(2,1)}, bf16[32,3072]{1,0:T(8,128)(2,1)}, bf16[32,3072]{1,0:T(8,128)(2,1)}, bf16[64,...) custom-call(s32[4]{0:T(128)} %pad_add_fusion.here_ref, ...), custom_call_target="tpu_custom_call" | custom-call | flops 2000000000 | bytes 10000000 | tf_op jit(solution)/shard_map/attention/pallas_call | solution.py:227
  59.5 2.0 %collective-permute-start.12 = (bf16[32,3072]{1,0:T(8,128)(2,1)}, bf16[32,3072]{1,0:T(8,128)(2,1)S(1)}, u32[]{:S(2)}, u32[]{:S(2)}) collective-permute-start(bf16[32,3072]{1,0:T(8,128)(2,1)} %get-tuple-element.33), channel_id=1, source_target_pairs={{0,1},{1,2},{2,3},{3,4},{4,5},{5,6},{6,7},{7,0},{8,9},{9,10},{10,1... | collective-permute-start | bytes 589832 | tf_op jit(solution)/shard_map/ppermute | solution.py:302
  61.5 4.0 %collective-permute-start.22 = (bf16[32,3072]{1,0:T(8,128)(2,1)}, bf16[32,3072]{1,0:T(8,128)(2,1)S(1)}, u32[]{:S(2)}, u32[]{:S(2)}) collective-permute-start(bf16[32,3072]{1,0:T(8,128)(2,1)} %get-tuple-element.38), channel_id=1, source_target_pairs={{0,7},{1,0},{2,1},{3,2},{4,3},{5,4},{6,5},{7,6},{8,15},{9,8},{10,9... | collective-permute-start | bytes 589832 | tf_op jit(solution)/shard_map/ppermute | solution.py:302
  65.6 3.2 %collective-permute-start.19 = (bf16[32,3072]{1,0:T(8,128)(2,1)}, bf16[32,3072]{1,0:T(8,128)(2,1)S(1)}, u32[]{:S(2)}, u32[]{:S(2)}) collective-permute-start(bf16[32,3072]{1,0:T(8,128)(2,1)} %get-tuple-element.37), channel_id=1, source_target_pairs={{0,7},{1,0},{2,1},{3,2},{4,3},{5,4},{6,5},{7,6},{8,15},{9,8},{10,9... | collective-permute-start | bytes 589832 | tf_op jit(solution)/shard_map/ppermute | solution.py:302
  68.8 2.6 %collective-permute-done.12 = bf16[32,3072]{1,0:T(8,128)(2,1)S(1)} collective-permute-done((bf16[32,3072]{1,0:T(8,128)(2,1)}, bf16[32,3072]{1,0:T(8,128)(2,1)S(1)}, u32[]{:S(2)}, u32[]{:S(2)}) %collective-permute-start.12) | collective-permute-done | bytes 196640 | tf_op jit(solution)/shard_map/ppermute | solution.py:302
  71.4 1.1 %add_convert_fusion.3 = (bf16[32,3072]{1,0:T(8,128)(2,1)S(1)}, bf16[32,3072]{1,0:T(8,128)(2,1)S(1)}) fusion(bf16[32,3072]{1,0:T(8,128)(2,1)S(1)} %collective-permute-done.22, bf16[64,3072]{1,0:T(8,128)(2,1)} %get-tuple-element.32, bf16[32,3072]{1,0:T(8,128)(2,1)S(1)} %collective-permute-done.12), kind=kLoop, calls=%fused_computation.4 | loop fusion | flops 786432 | bytes 1179648 | tf_op jit(solution)/shard_map/convert_element_type | solution.py:301
  72.6 3.4 %collective-permute-start.23 = (bf16[32,3072]{1,0:T(8,128)(2,1)S(1)}, bf16[32,3072]{1,0:T(8,128)(2,1)S(1)}, u32[]{:S(2)}, u32[]{:S(2)}) collective-permute-start(bf16[32,3072]{1,0:T(8,128)(2,1)S(1)} %get-tuple-element.47), channel_id=1, source_target_pairs={{0,7},{1,0},{2,1},{3,2},{4,3},{5,4},{6,5},{7,6},{8,15},{9,8},{10,9... | collective-permute-start | bytes 589832 | tf_op jit(solution)/shard_map/ppermute | solution.py:302
  76.0 1.1 %add_convert_fusion.5 = (bf16[32,3072]{1,0:T(8,128)(2,1)S(1)}, bf16[32,3072]{1,0:T(8,128)(2,1)S(1)}) fusion(bf16[32,3072]{1,0:T(8,128)(2,1)S(1)} %collective-permute-done.19, bf16[64,3072]{1,0:T(8,128)(2,1)} %get-tuple-element.35, bf16[32,3072]{1,0:T(8,128)(2,1)S(1)} %collective-permute-done.16), kind=kLoop, calls=%fused_computation.6 | loop fusion | flops 786432 | bytes 1179648 | tf_op jit(solution)/shard_map/convert_element_type | solution.py:301
  77.1 3.3 %collective-permute-start.20 = (bf16[32,3072]{1,0:T(8,128)(2,1)S(1)}, bf16[32,3072]{1,0:T(8,128)(2,1)S(1)}, u32[]{:S(2)}, u32[]{:S(2)}) collective-permute-start(bf16[32,3072]{1,0:T(8,128)(2,1)S(1)} %get-tuple-element.41), channel_id=1, source_target_pairs={{0,7},{1,0},{2,1},{3,2},{4,3},{5,4},{6,5},{7,6},{8,15},{9,8},{10,9... | collective-permute-start | bytes 589832 | tf_op jit(solution)/shard_map/ppermute | solution.py:302
  80.4 2.8 %collective-permute-done.13 = bf16[32,3072]{1,0:T(8,128)(2,1)S(1)} collective-permute-done((bf16[32,3072]{1,0:T(8,128)(2,1)S(1)}, bf16[32,3072]{1,0:T(8,128)(2,1)S(1)}, u32[]{:S(2)}, u32[]{:S(2)}) %collective-permute-start.13) | collective-permute-done | bytes 196640 | tf_op jit(solution)/shard_map/ppermute | solution.py:302
  83.2 1.1 %add_convert_fusion.2 = (bf16[32,3072]{1,0:T(8,128)(2,1)S(1)}, bf16[32,3072]{1,0:T(8,128)(2,1)S(1)}) fusion(bf16[32,3072]{1,0:T(8,128)(2,1)S(1)} %collective-permute-done.23, bf16[64,3072]{1,0:T(8,128)(2,1)} %get-tuple-element.31, bf16[32,3072]{1,0:T(8,128)(2,1)S(1)} %collective-permute-done.13), kind=kLoop, calls=%fused_computation.3 | loop fusion | flops 786432 | bytes 1179648 | tf_op jit(solution)/shard_map/convert_element_type | solution.py:301
  84.8 1.6 %collective-permute-start.14 = (bf16[32,3072]{1,0:T(8,128)(2,1)S(1)}, bf16[32,3072]{1,0:T(8,128)(2,1)S(1)}, u32[]{:S(2)}, u32[]{:S(2)}) collective-permute-start(bf16[32,3072]{1,0:T(8,128)(2,1)S(1)} %get-tuple-element.46), channel_id=1, source_target_pairs={{0,1},{1,2},{2,3},{3,4},{4,5},{5,6},{6,7},{7,0},{8,9},{9,10},{10,1... | collective-permute-start | bytes 589832 | tf_op jit(solution)/shard_map/ppermute | solution.py:302
  86.5 1.8 %collective-permute-done.17 = bf16[32,3072]{1,0:T(8,128)(2,1)S(1)} collective-permute-done((bf16[32,3072]{1,0:T(8,128)(2,1)S(1)}, bf16[32,3072]{1,0:T(8,128)(2,1)S(1)}, u32[]{:S(2)}, u32[]{:S(2)}) %collective-permute-start.17) | collective-permute-done | bytes 196640 | tf_op jit(solution)/shard_map/ppermute | solution.py:302
  88.2 1.1 %add_convert_fusion.4 = (bf16[32,3072]{1,0:T(8,128)(2,1)S(1)}, bf16[32,3072]{1,0:T(8,128)(2,1)S(1)}) fusion(bf16[32,3072]{1,0:T(8,128)(2,1)S(1)} %collective-permute-done.20, bf16[64,3072]{1,0:T(8,128)(2,1)} %get-tuple-element.34, bf16[32,3072]{1,0:T(8,128)(2,1)S(1)} %collective-permute-done.17), kind=kLoop, calls=%fused_computation.5 | loop fusion | flops 786432 | bytes 1179648 | tf_op jit(solution)/shard_map/convert_element_type | solution.py:301
  89.5 2.0 %collective-permute-start.18 = (bf16[32,3072]{1,0:T(8,128)(2,1)S(1)}, bf16[32,3072]{1,0:T(8,128)(2,1)S(1)}, u32[]{:S(2)}, u32[]{:S(2)}) collective-permute-start(bf16[32,3072]{1,0:T(8,128)(2,1)S(1)} %get-tuple-element.40), channel_id=1, source_target_pairs={{0,1},{1,2},{2,3},{3,4},{4,5},{5,6},{6,7},{7,0},{8,9},{9,10},{10,1... | collective-permute-start | bytes 589832 | tf_op jit(solution)/shard_map/ppermute | solution.py:302
  91.7 1.6 %collective-permute-done.14 = bf16[32,3072]{1,0:T(8,128)(2,1)S(1)} collective-permute-done((bf16[32,3072]{1,0:T(8,128)(2,1)S(1)}, bf16[32,3072]{1,0:T(8,128)(2,1)S(1)}, u32[]{:S(2)}, u32[]{:S(2)}) %collective-permute-start.14) | collective-permute-done | bytes 196640 | tf_op jit(solution)/shard_map/ppermute | solution.py:302
  93.4 2.0 %collective-permute-start.15 = (bf16[32,3072]{1,0:T(8,128)(2,1)S(1)}, bf16[32,3072]{1,0:T(8,128)(2,1)S(1)}, u32[]{:S(2)}, u32[]{:S(2)}) collective-permute-start(bf16[32,3072]{1,0:T(8,128)(2,1)S(1)} %get-tuple-element.44), channel_id=1, source_target_pairs={{0,1},{1,2},{2,3},{3,4},{4,5},{5,6},{6,7},{7,0},{8,9},{9,10},{10,1... | collective-permute-start | bytes 589832 | tf_op jit(solution)/shard_map/ppermute | solution.py:302
  95.5 1.0 collective-permute-done.21
  96.4 1.6 %collective-permute-done.18 = bf16[32,3072]{1,0:T(8,128)(2,1)S(1)} collective-permute-done((bf16[32,3072]{1,0:T(8,128)(2,1)S(1)}, bf16[32,3072]{1,0:T(8,128)(2,1)S(1)}, u32[]{:S(2)}, u32[]{:S(2)}) %collective-permute-start.18) | collective-permute-done | bytes 196640 | tf_op jit(solution)/shard_map/ppermute | solution.py:302
  98.0 1.0 %collective-permute-done.25 = bf16[32,3072]{1,0:T(8,128)(2,1)S(1)} collective-permute-done((bf16[32,3072]{1,0:T(8,128)(2,1)S(1)}, bf16[32,3072]{1,0:T(8,128)(2,1)S(1)}, u32[]{:S(2)}, u32[]{:S(2)}) %collective-permute-start.25) | collective-permute-done | bytes 196640 | tf_op jit(solution)/shard_map/ppermute | solution.py:302
  99.1 1.6 %collective-permute-done.15 = bf16[32,3072]{1,0:T(8,128)(2,1)S(1)} collective-permute-done((bf16[32,3072]{1,0:T(8,128)(2,1)S(1)}, bf16[32,3072]{1,0:T(8,128)(2,1)S(1)}, u32[]{:S(2)}, u32[]{:S(2)}) %collective-permute-start.15) | collective-permute-done | bytes 196640 | tf_op jit(solution)/shard_map/ppermute | solution.py:302
  100.7 0.9 add_convert_fusion
  (68 shorter events, 6.8 us)
Async XLA Ops:
  1.0 6.3 %collective-permute-start.2 = (bf16[256,256]{1,0:T(8,128)(2,1)S(1)}, bf16[256,256]{1,0:T(8,128)(2,1)S(1)}, u32[]{:S(2)}, u32[]{:S(2)}) collective-permute-start(bf16[256,256]{1,0:T(8,128)(2,1)S(1)} %pad_maximum_fusion), channel_id=1, source_target_pairs={{0,48},{8,200},{16,0},{24,216},{32,16},{40,232},{48,32},{56,248},{... | collective-permute-start | bytes 393224 | tf_op jit(solution)/shard_map/ppermute | solution.py:269
  1.9 7.2 %collective-permute-start.1 = (bf16[256,256]{1,0:T(8,128)(2,1)S(1)}, bf16[256,256]{1,0:T(8,128)(2,1)S(1)}, u32[]{:S(2)}, u32[]{:S(2)}) collective-permute-start(bf16[256,256]{1,0:T(8,128)(2,1)S(1)} %pad_maximum_fusion), channel_id=1, source_target_pairs={{0,32},{8,136},{16,48},{24,152},{32,0},{40,168},{48,16},{56,184},{... | collective-permute-start | bytes 393224 | tf_op jit(solution)/shard_map/ppermute | solution.py:269
  4.7 5.0 %collective-permute-start = (bf16[256,256]{1,0:T(8,128)(2,1)S(1)}, bf16[256,256]{1,0:T(8,128)(2,1)S(1)}, u32[]{:S(2)}, u32[]{:S(2)}) collective-permute-start(bf16[256,256]{1,0:T(8,128)(2,1)S(1)} %pad_maximum_fusion), channel_id=1, source_target_pairs={{0,16},{8,72},{16,32},{24,88},{32,48},{40,104},{48,0},{56,120},{64... | collective-permute-start | bytes 393224 | tf_op jit(solution)/shard_map/ppermute | solution.py:269
  9.7 35.8 %copy-start.3 = (bf16[1024,256]{1,0:T(8,128)(2,1)}, bf16[1024,256]{1,0:T(8,128)(2,1)S(1)}, u32[]{:S(2)}) copy-start(bf16[1024,256]{1,0:T(8,128)(2,1)S(1)} %constant_dynamic-update-slice_fusion.refs_0_) | copy-start | bytes 1572868
  9.7 9.6 %collective-permute-start.4 = (bf16[1024,256]{1,0:T(8,128)(2,1)S(1)}, bf16[1024,256]{1,0:T(8,128)(2,1)S(1)}, u32[]{:S(2)}, u32[]{:S(2)}) collective-permute-start(bf16[1024,256]{1,0:T(8,128)(2,1)S(1)} %constant_dynamic-update-slice_fusion.refs_0_), channel_id=1, source_target_pairs={{0,192},{8,56},{16,208},{24,8},{32,224},{40,24},{48,240},{56,40},{... | collective-permute-start | bytes 1572872 | tf_op jit(solution)/shard_map/ppermute | solution.py:269
  12.6 10.5 %collective-permute-start.3 = (bf16[1024,256]{1,0:T(8,128)(2,1)S(1)}, bf16[1024,256]{1,0:T(8,128)(2,1)S(1)}, u32[]{:S(2)}, u32[]{:S(2)}) collective-permute-start(bf16[1024,256]{1,0:T(8,128)(2,1)S(1)} %constant_dynamic-update-slice_fusion.refs_0_), channel_id=1, source_target_pairs={{0,64},{8,24},{16,80},{24,40},{32,96},{40,56},{48,112},{56,8},{64,... | collective-permute-start | bytes 1572872 | tf_op jit(solution)/shard_map/ppermute | solution.py:269
  12.6 31.4 %collective-permute-start.7 = (bf16[1024,256]{1,0:T(8,128)(2,1)S(1)}, bf16[1024,256]{1,0:T(8,128)(2,1)S(1)}, u32[]{:S(2)}, u32[]{:S(2)}) collective-permute-start(bf16[1024,256]{1,0:T(8,128)(2,1)S(1)} %constant_dynamic-update-slice_fusion.refs_0_), channel_id=1, source_target_pairs={{0,8},{8,0},{16,24},{24,16},{32,40},{40,32},{48,56},{56,48},{64,72... | collective-permute-start | bytes 1572872 | tf_op jit(solution)/shard_map/ppermute | solution.py:269
  19.3 26.2 %copy-start.1 = (bf16[1024,256]{1,0:T(8,128)(2,1)}, bf16[1024,256]{1,0:T(8,128)(2,1)S(1)}, u32[]{:S(2)}) copy-start(bf16[1024,256]{1,0:T(8,128)(2,1)S(1)} %collective-permute-done.4.refs_2_) | copy-start | bytes 1572868
  19.4 7.7 %collective-permute-start.6 = (bf16[512,256]{1,0:T(8,128)(2,1)S(1)}, bf16[512,256]{1,0:T(8,128)(2,1)S(1)}, u32[]{:S(2)}, u32[]{:S(2)}) collective-permute-start(bf16[512,256]{1,0:T(8,128)(2,1)S(1)} %slice.51), channel_id=1, source_target_pairs={{0,192},{8,56},{16,208},{24,8},{32,224},{40,24},{48,240},{56,40},{... | collective-permute-start | bytes 786440 | tf_op jit(solution)/shard_map/ppermute | solution.py:269
  23.1 20.9 %collective-permute-start.9 = (bf16[1024,256]{1,0:T(8,128)(2,1)S(1)}, bf16[1024,256]{1,0:T(8,128)(2,1)S(1)}, u32[]{:S(2)}, u32[]{:S(2)}) collective-permute-start(bf16[1024,256]{1,0:T(8,128)(2,1)S(1)} %collective-permute-done.4.refs_2_), channel_id=1, source_target_pairs={{0,8},{8,0},{16,24},{24,16},{32,40},{40,32},{48,56},{56,48},{64,72... | collective-permute-start | bytes 1572872 | tf_op jit(solution)/shard_map/ppermute | solution.py:269
  23.1 22.4 %copy-start.2 = (bf16[1024,256]{1,0:T(8,128)(2,1)}, bf16[1024,256]{1,0:T(8,128)(2,1)S(1)}, u32[]{:S(2)}) copy-start(bf16[1024,256]{1,0:T(8,128)(2,1)S(1)} %collective-permute-done.3.refs_1_) | copy-start | bytes 1572868
  23.2 20.9 %collective-permute-start.8 = (bf16[1024,256]{1,0:T(8,128)(2,1)S(1)}, bf16[1024,256]{1,0:T(8,128)(2,1)S(1)}, u32[]{:S(2)}, u32[]{:S(2)}) collective-permute-start(bf16[1024,256]{1,0:T(8,128)(2,1)S(1)} %collective-permute-done.3.refs_1_), channel_id=1, source_target_pairs={{0,8},{8,0},{16,24},{24,16},{32,40},{40,32},{48,56},{56,48},{64,72... | collective-permute-start | bytes 1572872 | tf_op jit(solution)/shard_map/ppermute | solution.py:269
  23.8 7.6 %collective-permute-start.5 = (bf16[512,256]{1,0:T(8,128)(2,1)S(1)}, bf16[512,256]{1,0:T(8,128)(2,1)S(1)}, u32[]{:S(2)}, u32[]{:S(2)}) collective-permute-start(bf16[512,256]{1,0:T(8,128)(2,1)S(1)} %slice.50), channel_id=1, source_target_pairs={{0,64},{8,24},{16,80},{24,40},{32,96},{40,56},{48,112},{56,8},{64,... | collective-permute-start | bytes 786440 | tf_op jit(solution)/shard_map/ppermute | solution.py:269
  27.0 17.0 %collective-permute-start.11 = (bf16[512,256]{1,0:T(8,128)(2,1)S(1)}, bf16[512,256]{1,0:T(8,128)(2,1)S(1)}, u32[]{:S(2)}, u32[]{:S(2)}) collective-permute-start(bf16[512,256]{1,0:T(8,128)(2,1)S(1)} %collective-permute-done.6.refs_4_), channel_id=1, source_target_pairs={{0,8},{8,0},{16,24},{24,16},{32,40},{40,32},{48,56},{56,48},{64,72... | collective-permute-start | bytes 786440 | tf_op jit(solution)/shard_map/ppermute | solution.py:269
  31.3 12.7 %collective-permute-start.10 = (bf16[512,256]{1,0:T(8,128)(2,1)S(1)}, bf16[512,256]{1,0:T(8,128)(2,1)S(1)}, u32[]{:S(2)}, u32[]{:S(2)}) collective-permute-start(bf16[512,256]{1,0:T(8,128)(2,1)S(1)} %collective-permute-done.5.refs_3_), channel_id=1, source_target_pairs={{0,8},{8,0},{16,24},{24,16},{32,40},{40,32},{48,56},{56,48},{64,72... | collective-permute-start | bytes 786440 | tf_op jit(solution)/shard_map/ppermute | solution.py:269
  59.5 33.8 %copy-start.7 = (bf16[64,3072]{1,0:T(8,128)(2,1)S(1)}, bf16[64,3072]{1,0:T(8,128)(2,1)}, u32[]{:S(2)}) copy-start(bf16[64,3072]{1,0:T(8,128)(2,1)} %get-tuple-element.30) | copy-start | bytes 1179652
  59.5 41.2 %copy-start.12 = (bf16[32,3072]{1,0:T(8,128)(2,1)S(1)}, bf16[32,3072]{1,0:T(8,128)(2,1)}, u32[]{:S(2)}) copy-start(bf16[32,3072]{1,0:T(8,128)(2,1)} %get-tuple-element.28) | copy-start | bytes 589828
  59.5 41.2 %copy-start.13 = (bf16[32,3072]{1,0:T(8,128)(2,1)S(1)}, bf16[32,3072]{1,0:T(8,128)(2,1)}, u32[]{:S(2)}) copy-start(bf16[32,3072]{1,0:T(8,128)(2,1)} %get-tuple-element.29) | copy-start | bytes 589828
  59.5 11.9 %collective-permute-start.12 = (bf16[32,3072]{1,0:T(8,128)(2,1)}, bf16[32,3072]{1,0:T(8,128)(2,1)S(1)}, u32[]{:S(2)}, u32[]{:S(2)}) collective-permute-start(bf16[32,3072]{1,0:T(8,128)(2,1)} %get-tuple-element.33), channel_id=1, source_target_pairs={{0,1},{1,2},{2,3},{3,4},{4,5},{5,6},{6,7},{7,0},{8,9},{9,10},{10,1... | collective-permute-start | bytes 589832 | tf_op jit(solution)/shard_map/ppermute | solution.py:302
  61.5 9.9 %collective-permute-start.22 = (bf16[32,3072]{1,0:T(8,128)(2,1)}, bf16[32,3072]{1,0:T(8,128)(2,1)S(1)}, u32[]{:S(2)}, u32[]{:S(2)}) collective-permute-start(bf16[32,3072]{1,0:T(8,128)(2,1)} %get-tuple-element.38), channel_id=1, source_target_pairs={{0,7},{1,0},{2,1},{3,2},{4,3},{5,4},{6,5},{7,6},{8,15},{9,8},{10,9... | collective-permute-start | bytes 589832 | tf_op jit(solution)/shard_map/ppermute | solution.py:302
  65.6 10.4 %collective-permute-start.16 = (bf16[32,3072]{1,0:T(8,128)(2,1)}, bf16[32,3072]{1,0:T(8,128)(2,1)S(1)}, u32[]{:S(2)}, u32[]{:S(2)}) collective-permute-start(bf16[32,3072]{1,0:T(8,128)(2,1)} %get-tuple-element.36), channel_id=1, source_target_pairs={{0,1},{1,2},{2,3},{3,4},{4,5},{5,6},{6,7},{7,0},{8,9},{9,10},{10,1... | collective-permute-start | bytes 589832 | tf_op jit(solution)/shard_map/ppermute | solution.py:302
  65.6 10.4 %collective-permute-start.19 = (bf16[32,3072]{1,0:T(8,128)(2,1)}, bf16[32,3072]{1,0:T(8,128)(2,1)S(1)}, u32[]{:S(2)}, u32[]{:S(2)}) collective-permute-start(bf16[32,3072]{1,0:T(8,128)(2,1)} %get-tuple-element.37), channel_id=1, source_target_pairs={{0,7},{1,0},{2,1},{3,2},{4,3},{5,4},{6,5},{7,6},{8,15},{9,8},{10,9... | collective-permute-start | bytes 589832 | tf_op jit(solution)/shard_map/ppermute | solution.py:302
  72.6 7.8 %collective-permute-start.23 = (bf16[32,3072]{1,0:T(8,128)(2,1)S(1)}, bf16[32,3072]{1,0:T(8,128)(2,1)S(1)}, u32[]{:S(2)}, u32[]{:S(2)}) collective-permute-start(bf16[32,3072]{1,0:T(8,128)(2,1)S(1)} %get-tuple-element.47), channel_id=1, source_target_pairs={{0,7},{1,0},{2,1},{3,2},{4,3},{5,4},{6,5},{7,6},{8,15},{9,8},{10,9... | collective-permute-start | bytes 589832 | tf_op jit(solution)/shard_map/ppermute | solution.py:302
  76.0 7.3 %collective-permute-start.13 = (bf16[32,3072]{1,0:T(8,128)(2,1)S(1)}, bf16[32,3072]{1,0:T(8,128)(2,1)S(1)}, u32[]{:S(2)}, u32[]{:S(2)}) collective-permute-start(bf16[32,3072]{1,0:T(8,128)(2,1)S(1)} %get-tuple-element.48), channel_id=1, source_target_pairs={{0,1},{1,2},{2,3},{3,4},{4,5},{5,6},{6,7},{7,0},{8,9},{9,10},{10,1... | collective-permute-start | bytes 589832 | tf_op jit(solution)/shard_map/ppermute | solution.py:302
  77.1 9.4 %collective-permute-start.20 = (bf16[32,3072]{1,0:T(8,128)(2,1)S(1)}, bf16[32,3072]{1,0:T(8,128)(2,1)S(1)}, u32[]{:S(2)}, u32[]{:S(2)}) collective-permute-start(bf16[32,3072]{1,0:T(8,128)(2,1)S(1)} %get-tuple-element.41), channel_id=1, source_target_pairs={{0,7},{1,0},{2,1},{3,2},{4,3},{5,4},{6,5},{7,6},{8,15},{9,8},{10,9... | collective-permute-start | bytes 589832 | tf_op jit(solution)/shard_map/ppermute | solution.py:302
  80.4 7.8 %collective-permute-start.17 = (bf16[32,3072]{1,0:T(8,128)(2,1)S(1)}, bf16[32,3072]{1,0:T(8,128)(2,1)S(1)}, u32[]{:S(2)}, u32[]{:S(2)}) collective-permute-start(bf16[32,3072]{1,0:T(8,128)(2,1)S(1)} %get-tuple-element.42), channel_id=1, source_target_pairs={{0,1},{1,2},{2,3},{3,4},{4,5},{5,6},{6,7},{7,0},{8,9},{9,10},{10,1... | collective-permute-start | bytes 589832 | tf_op jit(solution)/shard_map/ppermute | solution.py:302
  84.4 7.3 %collective-permute-start.24 = (bf16[32,3072]{1,0:T(8,128)(2,1)S(1)}, bf16[32,3072]{1,0:T(8,128)(2,1)S(1)}, u32[]{:S(2)}, u32[]{:S(2)}) collective-permute-start(bf16[32,3072]{1,0:T(8,128)(2,1)S(1)} %get-tuple-element.45), channel_id=1, source_target_pairs={{0,7},{1,0},{2,1},{3,2},{4,3},{5,4},{6,5},{7,6},{8,15},{9,8},{10,9... | collective-permute-start | bytes 589832 | tf_op jit(solution)/shard_map/ppermute | solution.py:302
  84.8 8.4 %collective-permute-start.14 = (bf16[32,3072]{1,0:T(8,128)(2,1)S(1)}, bf16[32,3072]{1,0:T(8,128)(2,1)S(1)}, u32[]{:S(2)}, u32[]{:S(2)}) collective-permute-start(bf16[32,3072]{1,0:T(8,128)(2,1)S(1)} %get-tuple-element.46), channel_id=1, source_target_pairs={{0,1},{1,2},{2,3},{3,4},{4,5},{5,6},{6,7},{7,0},{8,9},{9,10},{10,1... | collective-permute-start | bytes 589832 | tf_op jit(solution)/shard_map/ppermute | solution.py:302
  89.4 7.1 %collective-permute-start.21 = (bf16[32,3072]{1,0:T(8,128)(2,1)S(1)}, bf16[32,3072]{1,0:T(8,128)(2,1)S(1)}, u32[]{:S(2)}, u32[]{:S(2)}) collective-permute-start(bf16[32,3072]{1,0:T(8,128)(2,1)S(1)} %get-tuple-element.39), channel_id=1, source_target_pairs={{0,7},{1,0},{2,1},{3,2},{4,3},{5,4},{6,5},{7,6},{8,15},{9,8},{10,9... | collective-permute-start | bytes 589832 | tf_op jit(solution)/shard_map/ppermute | solution.py:302
  89.5 8.6 %collective-permute-start.18 = (bf16[32,3072]{1,0:T(8,128)(2,1)S(1)}, bf16[32,3072]{1,0:T(8,128)(2,1)S(1)}, u32[]{:S(2)}, u32[]{:S(2)}) collective-permute-start(bf16[32,3072]{1,0:T(8,128)(2,1)S(1)} %get-tuple-element.40), channel_id=1, source_target_pairs={{0,1},{1,2},{2,3},{3,4},{4,5},{5,6},{6,7},{7,0},{8,9},{9,10},{10,1... | collective-permute-start | bytes 589832 | tf_op jit(solution)/shard_map/ppermute | solution.py:302
  93.3 5.7 %collective-permute-start.25 = (bf16[32,3072]{1,0:T(8,128)(2,1)S(1)}, bf16[32,3072]{1,0:T(8,128)(2,1)S(1)}, u32[]{:S(2)}, u32[]{:S(2)}) collective-permute-start(bf16[32,3072]{1,0:T(8,128)(2,1)S(1)} %get-tuple-element.43), channel_id=1, source_target_pairs={{0,7},{1,0},{2,1},{3,2},{4,3},{5,4},{6,5},{7,6},{8,15},{9,8},{10,9... | collective-permute-start | bytes 589832 | tf_op jit(solution)/shard_map/ppermute | solution.py:302
  93.4 7.3 %collective-permute-start.15 = (bf16[32,3072]{1,0:T(8,128)(2,1)S(1)}, bf16[32,3072]{1,0:T(8,128)(2,1)S(1)}, u32[]{:S(2)}, u32[]{:S(2)}) collective-permute-start(bf16[32,3072]{1,0:T(8,128)(2,1)S(1)} %get-tuple-element.44), channel_id=1, source_target_pairs={{0,1},{1,2},{2,3},{3,4},{4,5},{5,6},{6,7},{7,0},{8,9},{9,10},{10,1... | collective-permute-start | bytes 589832 | tf_op jit(solution)/shard_map/ppermute | solution.py:302
  (8 other events, 44.6 us)
